TPU v7x, 512 devices: a whole 4x8x8 slice. The times are simulated.
512 devices in a mesh: row: 32 (over z, y_lo, core), col: 16 (over x, y_hi).
Axes of the slice: x: 4, y: 8 (y_hi: 4, y_lo: 2; y = y_hi * 2 + y_lo), z: 8, core: 2. Of those that a mesh axis runs over, the one named last changes fastest.
Arguments:
- pair_exchange: bfloat16 [1024, 16, 1024], P(('row', 'col')), may hold values from -6 to 6
- conduction: bfloat16 [1024, 4, 1024], P(('row', 'col')), may hold values from -6 to 6
- valence: bfloat16 [1024, 4, 1024], P(('row', 'col')), may hold values from -6 to 6
- coulomb: float32 [1024], replicated, may hold values from 0.5 to 5
- screening: float32 [289, 1024], replicated, may hold values from 0.1 to 1
- energies: float32 [1024, 16], P(('row', 'col')), may hold values from 1 to 9
- vectors: bfloat16 [1024, 512], P(('row', 'col')), may hold values from -6 to 6
- k_coords: int32 [1024, 2], P(('row', 'col')), may hold values from 0 to 31, as said below
Outputs:
- residual_block: float32 [1024, 512], P(('row', 'col'))
- alpha: float32 [32, 32], replicated
Inputs may be any that keep to these rules, and one draw needn't show every extreme that they name: `k_coords`: each row holds a k-point's coordinates on the periodic 32 x 32 mesh, first then second; every mesh point occurs exactly once.
All inputs are finite; a program needn't handle non-finite values.
Results may differ from a plain program's by a relative error of at most 0.0028.
Values may be sent and summed in bfloat16 or wider, within the bound.
No kernel may reach another device: no remote copies, remote signals or barrier semaphores. Data moves between devices by JAX's collectives and lax.ppermute only.
A program may use at most 64 MiB of HBM per device.

v0:
```python
import functools

import jax
import jax.numpy as jnp
from jax import lax
from jax.sharding import Mesh
from jax.sharding import PartitionSpec as P

MX = 32
ROW = ("row_0", "row_1", "row_2")
COL = ("col_0", "col_1")
ROW_COL = ("row_0", "row_1", "row_2", "col_0", "col_1")


highest = lax.Precision.HIGHEST


def over_axes(x, axes):
    return functools.reduce(lax.psum, axes, x)


def pair_factors(conduction, valence):
    count, valence_count, plane_count = valence.shape
    joined = (
        valence.astype(jnp.float32)[:, :, None, :] * conduction.astype(jnp.float32)[:, None, :, :]
    )
    return joined.reshape(count, valence_count * conduction.shape[1], plane_count).astype(
        jnp.bfloat16
    )


def transfer_index(rows_at, cols_at, mesh_cols):
    delta_first = jnp.mod(rows_at[:, None, 0] - cols_at[None, :, 0], MX)
    delta_second = jnp.mod(rows_at[:, None, 1] - cols_at[None, :, 1], mesh_cols)
    fold_first = jnp.minimum(delta_first, MX - delta_first)
    fold_second = jnp.minimum(delta_second, mesh_cols - delta_second)
    return (fold_first * (mesh_cols // 2 + 1) + fold_second).astype(jnp.int32)


def on_device(pair_exchange, conduction, valence, coulomb, screening, energies, vectors, k_coords):
    local_count, band_count, plane_count = pair_exchange.shape
    vector_count = vectors.shape[1] // band_count
    row_count = lax.axis_size(ROW)
    col_count = lax.axis_size(COL)
    total_count = local_count * row_count * col_count
    mesh_cols = total_count // MX
    moving = vectors.reshape(local_count, band_count, vector_count)
    partial_density = jnp.einsum(
        "ktg,ktn->gn", pair_exchange, moving, preferred_element_type=jnp.float32
    )
    density = lax.psum(partial_density, ROW_COL)
    block_size = 128
    sweeps = plane_count // block_size
    col_cond, col_val, col_vec, col_at = (
        lax.all_gather(conduction, ROW, axis=0, tiled=True),
        lax.all_gather(valence, ROW, axis=0, tiled=True),
        lax.all_gather(vectors, ROW, axis=0, tiled=True),
        lax.all_gather(k_coords, ROW, axis=0, tiled=True),
    )
    row_cond, row_val, row_at = (
        lax.all_gather(conduction, COL, axis=0, tiled=True),
        lax.all_gather(valence, COL, axis=0, tiled=True),
        lax.all_gather(k_coords, COL, axis=0, tiled=True),
    )
    row_pairs = pair_factors(row_cond, row_val)
    col_pairs = pair_factors(col_cond, col_val)
    indices = transfer_index(row_at, col_at, mesh_cols)
    col_moving = col_vec.reshape(-1, band_count, vector_count)

    def square_sweep(sweep_index, running):
        anchor = sweep_index * block_size
        coupling = jnp.take(
            lax.dynamic_slice_in_dim(screening, anchor, block_size, 1), indices, axis=0
        )
        row_block = lax.dynamic_slice_in_dim(row_pairs, anchor, block_size, 2)
        col_block = lax.dynamic_slice_in_dim(col_pairs, anchor, block_size, 2)
        col_proj = jnp.einsum(
            "ktg,ktn->kng", col_block, col_moving, preferred_element_type=jnp.float32
        )
        potential = jnp.einsum("ijg,jng->ing", coupling, col_proj, precision=highest)
        return running + jnp.einsum(
            "ktg,kng->ktn", row_block.astype(jnp.float32), potential, precision=highest
        )

    forward = lax.fori_loop(
        0,
        sweeps,
        square_sweep,
        jnp.zeros((row_pairs.shape[0], band_count, vector_count), jnp.float32),
    )
    owned = lax.psum_scatter(
        forward.reshape(col_count, local_count, band_count, vector_count),
        COL,
        scatter_dimension=0,
        tiled=True,
    )[0]
    moving_wide = moving.astype(jnp.float32)
    exchange_term = jnp.einsum(
        "ktg,gn->ktn", pair_exchange.astype(jnp.float32) * coulomb, density, precision=highest
    )
    applied = (
        energies[:, :, None] * moving_wide
        + 2.0 / (total_count * band_count) * exchange_term
        - owned / total_count
    )
    gram = jnp.einsum("ktm,ktn->mn", moving_wide, applied, precision=highest)
    alpha = over_axes(gram, ROW_COL) / (total_count * band_count)
    residual = applied - jnp.einsum("ktm,mn->ktn", moving_wide, alpha, precision=highest)
    return (residual.reshape(local_count, band_count * vector_count), alpha)


def solution(mesh):
    split = Mesh(mesh.devices.reshape(8, 2, 2, 4, 4), ("row_0", "row_1", "row_2", "col_0", "col_1"))
    return jax.shard_map(
        on_device,
        mesh=split,
        in_specs=(
            P(ROW_COL, None, None),
            P(ROW_COL, None, None),
            P(ROW_COL, None, None),
            P(),
            P(),
            P(ROW_COL, None),
            P(ROW_COL, None),
            P(ROW_COL, None),
        ),
        out_specs=(P(ROW_COL, None), P()),
        check_vma=False,
    )
```

profile of v0, /device:TPU:1, one launch (start us, length us, event | category | flops | bytes accessed | tf_op | source)
XLA Modules:
  0.0 623.2 jit_solution(7728930901200443616)
XLA Ops:
  8.8 1.7 convolution_bitcast_fusion.1
  10.6 42.1 %all-gather.2 = s32[32,2,2]{2,1,0:T(2,128)S(1)} all-gather(s32[1,2,2]{2,1,0:T(2,128)} %bitcast.67), channel_id=1, replica_groups=mesh['row_0'=8,'row_1'=2,'row_2'=2,'col_0'=4,'col_1'=4] {'row_0','row_1'..., dimensions={0}, use_global_device_ids=true | all-gather | bytes 528 | tf_op jit(solution)/shard_map/all_gather | solution.py:58
  52.7 36.6 %all-gather.1 = s32[16,2,2]{2,1,0:T(2,128)S(1)} all-gather(s32[1,2,2]{2,1,0:T(2,128)} %bitcast.68), channel_id=1, replica_groups=mesh['row_0'=8,'row_1'=2,'row_2'=2,'col_0'=4,'col_1'=4] {'col_0','col_1'}, dimensions={0}, use_global_device_ids=true | all-gather | bytes 272 | tf_op jit(solution)/shard_map/all_gather | solution.py:63
  89.2 40.1 %all_gather.23 = bf16[64,4,1024]{2,1,0:T(4,128)(2,1)S(1)} all-gather(bf16[2,4,1024]{2,1,0:T(4,128)(2,1)} %param.12), channel_id=1, replica_groups=mesh['row_0'=8,'row_1'=2,'row_2'=2,'col_0'=4,'col_1'=4] {'row_0','row_1'..., dimensions={0}, use_global_device_ids=true | all-gather | bytes 540672 | tf_op jit(solution)/shard_map/all_gather | solution.py:56
  129.4 33.0 %all_gather.21 = bf16[32,4,1024]{2,1,0:T(4,128)(2,1)S(1)} all-gather(bf16[2,4,1024]{2,1,0:T(4,128)(2,1)} %param.12), channel_id=1, replica_groups=mesh['row_0'=8,'row_1'=2,'row_2'=2,'col_0'=4,'col_1'=4] {'col_0','col_1'}, dimensions={0}, use_global_device_ids=true | all-gather | bytes 278528 | tf_op jit(solution)/shard_map/all_gather | solution.py:62
  162.3 41.2 %all_gather.24 = bf16[64,4,1024]{2,1,0:T(4,128)(2,1)S(1)} all-gather(bf16[2,4,1024]{2,1,0:T(4,128)(2,1)} %param.11), channel_id=1, replica_groups=mesh['row_0'=8,'row_1'=2,'row_2'=2,'col_0'=4,'col_1'=4] {'row_0','row_1'..., dimensions={0}, use_global_device_ids=true | all-gather | bytes 540672 | tf_op jit(solution)/shard_map/all_gather | solution.py:55
  203.5 36.0 %all_gather.22 = bf16[32,4,1024]{2,1,0:T(4,128)(2,1)S(1)} all-gather(bf16[2,4,1024]{2,1,0:T(4,128)(2,1)} %param.11), channel_id=1, replica_groups=mesh['row_0'=8,'row_1'=2,'row_2'=2,'col_0'=4,'col_1'=4] {'col_0','col_1'}, dimensions={0}, use_global_device_ids=true | all-gather | bytes 278528 | tf_op jit(solution)/shard_map/all_gather | solution.py:61
  240.2 1.5 multiply_convert_fusion
  241.7 2.1 convert_element_type.42
  245.7 37.8 %all-gather = bf16[32,2,512]{2,1,0:T(2,128)(2,1)S(1)} all-gather(bf16[1,2,512]{2,1,0:T(2,128)(2,1)S(1)} %bitcast.66), channel_id=1, replica_groups=mesh['row_0'=8,'row_1'=2,'row_2'=2,'col_0'=4,'col_1'=4] {'row_0','row_1'..., dimensions={0}, use_global_device_ids=true | all-gather | bytes 67584 | tf_op jit(solution)/shard_map/all_gather | solution.py:57
  283.7 178.4 %while.14 = (s32[]{:T(128)}, f32[32,16,32]{2,1,0:T(8,128)S(1)}, bf16[32,16,1024]{2,1,0:T(8,128)(2,1)}, bf16[64,16,1024]{2,1,0:T(8,128)(2,1)}, bf16[64,16,32]{2,1...) while((s32[]{:T(128)}, f32[32,16,32]{2,1,0:T(8,128)S(1)}, ...), condition=%wide.region_2.3_spmd.clone, body=%wide.region_1.2_spmd.clone.sunk | while | flops 134656000 | bytes 12475081 | solution.py:85
  284.8 5.5 gather_fusion
  290.3 2.8 copy.37
  294.4 2.9 copy.36
  297.4 5.7 fusion.49
  303.1 1.4 copy.38
  304.5 1.4 convolution_add_fusion.2
  307.1 5.5 gather_fusion
  312.6 2.8 copy.37
  316.7 2.9 copy.36
  319.7 5.7 fusion.49
  325.4 1.4 copy.38
  326.8 1.4 convolution_add_fusion.2
  329.4 5.5 gather_fusion
  334.9 2.8 copy.37
  339.0 2.9 copy.36
  342.0 5.7 fusion.49
  347.7 1.4 copy.38
  349.1 1.4 convolution_add_fusion.2
  351.7 5.5 gather_fusion
  357.1 2.8 copy.37
  361.3 2.9 copy.36
  364.3 5.7 fusion.49
  370.0 1.4 copy.38
  371.4 1.4 convolution_add_fusion.2
  374.0 5.5 gather_fusion
  379.5 2.8 copy.37
  383.6 2.9 copy.36
  386.6 5.7 fusion.49
  392.3 1.4 copy.38
  393.7 1.4 convolution_add_fusion.2
  396.3 5.5 gather_fusion
  401.7 2.8 copy.37
  405.9 2.9 copy.36
  408.9 5.7 fusion.49
  414.6 1.4 copy.38
  416.0 1.4 convolution_add_fusion.2
  418.6 5.5 gather_fusion
  424.0 2.8 copy.37
  428.2 2.9 copy.36
  431.2 5.7 fusion.49
  438.3 1.4 convolution_add_fusion.2
  440.9 5.5 gather_fusion
  446.3 2.8 copy.37
  450.5 2.9 copy.36
  453.5 5.7 fusion.49
  459.2 1.4 copy.38
  460.6 1.4 convolution_add_fusion.2
  462.8 79.4 %reduce-scatter.2.cloned.1.call-done = f32[1,2,16,32]{3,2,1,0:T(8,128)} async-done(((f32[16,2,16,32]{3,2,1,0:T(8,128)}), f32[1,2,16,32]{3,2,1,0:T(8,128)}) %reduce-scatter.2.cloned.1.call-update) | async-done | bytes 4112 | tf_op jit(solution)/shard_map/reduce_scatter | solution.py:91
  543.6 23.6 %psum.43 = f32[32,32]{0,1:T(8,128)S(1)} all-reduce(f32[32,32]{0,1:T(8,128)S(1)} %convolution_bitcast_fusion.3), channel_id=1, replica_groups=mesh['row_0'=8,'row_1'=2,'row_2'=2,'col_0'=4,'col_1'=4] {'row_0'}, use_global_device_ids=true, to_apply=%region_4.5 | all-reduce | flops 1024 | bytes 8192 | tf_op jit(solution)/shard_map/psum | solution.py:19
  567.2 5.5 psum.44
  572.6 14.9 %psum.45 = f32[32,32]{0,1:T(8,128)S(1)} all-reduce(f32[32,32]{0,1:T(8,128)S(1)} %psum.44), channel_id=1, replica_groups=mesh['row_0'=8,'row_1'=2,'row_2'=2,'col_0'=4,'col_1'=4] {'row_2'}, use_global_device_ids=true, to_apply=%region_6.7 | all-reduce | flops 1024 | bytes 8192 | tf_op jit(solution)/shard_map/psum | solution.py:19
  587.5 12.2 %psum.46 = f32[32,32]{0,1:T(8,128)S(1)} all-reduce(f32[32,32]{0,1:T(8,128)S(1)} %psum.45), channel_id=1, replica_groups=mesh['row_0'=8,'row_1'=2,'row_2'=2,'col_0'=4,'col_1'=4] {'col_0'}, use_global_device_ids=true, to_apply=%region_7.8 | all-reduce | flops 1024 | bytes 8192 | tf_op jit(solution)/shard_map/psum | solution.py:19
  599.7 14.5 %psum.47 = f32[32,32]{0,1:T(8,128)S(1)} all-reduce(f32[32,32]{0,1:T(8,128)S(1)} %psum.46), channel_id=1, replica_groups=mesh['row_0'=8,'row_1'=2,'row_2'=2,'col_0'=4,'col_1'=4] {'col_1'}, use_global_device_ids=true, to_apply=%region_8.9 | all-reduce | flops 1024 | bytes 8192 | tf_op jit(solution)/shard_map/psum | solution.py:19
  (85 shorter events, 28.6 us)
Async XLA Ops:
  8.0 454.8 %all-reduce.2.cloned.1.call-start = ((), (), s32[]{:S(2)}) async-start(), calls=%async_computation.1 | async-start | bytes 262144 | tf_op jit(solution)/shard_map/psum | solution.py:51
  10.5 531.7 %reduce-scatter.2.cloned.1.call-start = ((), (), s32[]{:S(2)}) async-start(), calls=%async_computation.2 | async-start | bytes 278528 | tf_op jit(solution)/shard_map/reduce_scatter | solution.py:91
  243.9 1.7 copy-start.2
  283.6 258.6 %copy-start.1 = (bf16[2,16,1024]{2,1,0:T(8,128)(2,1)S(1)}, bf16[2,16,1024]{2,1,0:T(8,128)(2,1)}, u32[]{:S(2)}) copy-start(bf16[2,16,1024]{2,1,0:T(8,128)(2,1)} %param.10) | copy-start | bytes 196612
  283.6 258.6 %copy-start.3 = (f32[1024]{0:T(1024)S(1)}, f32[1024]{0:T(1024)}, u32[]{:S(2)}) copy-start(f32[1024]{0:T(1024)} %param.13) | copy-start | bytes 12292
  283.6 258.6 %copy-start.4 = (f32[2,16]{1,0:T(2,128)S(1)}, f32[2,16]{1,0:T(2,128)}, u32[]{:S(2)}) copy-start(f32[2,16]{1,0:T(2,128)} %param.15) | copy-start | bytes 388
  462.1 0.7 copy-start
Sparse Core Ops, SparseCore 0:
  13.8 271.8 all-reduce.1
Sparse Core Ops, SparseCore 1:
  462.9 79.3 reduce-scatter.1
where the time goes:
time: 630 us; the launch traced here: 623 us
  blocking collectives  337 us (53%)
  local copies, waits for them, and re-layouts  115 us (18%)
  waiting for transfers between devices  79.5 us (13%)
  matrix products  70.7 us (11%)
  between operations  15.6 us (2%)
    reduce_scatter x1, waiting for transfers between devices, on_device(): lax.psum_scatter(forward.reshape(col_count, local_count, band_count, vect...  79.4 us
    psum x5, blocking collectives, over_axes(): return functools.reduce(lax.psum, axes, x)  70.7 us
    gather x16, local copies, waits for them, and re-layouts, square_sweep(): jnp.take(lax.dynamic_slice_in_dim(screening, anchor, block_size, 1), indi...  66.3 us
    dot_general x8, matrix products, square_sweep(): jnp.einsum('ijg,jng->ing', coupling, col_proj, precision=highest)  45.6 us
    all_gather x1, blocking collectives, on_device(): lax.all_gather(k_coords, ROW, axis=0, tiled=True)  42.1 us
    all_gather x1, blocking collectives, on_device(): lax.all_gather(conduction, ROW, axis=0, tiled=True)  41.2 us
    all_gather x1, blocking collectives, on_device(): lax.all_gather(valence, ROW, axis=0, tiled=True)  40.1 us
    all_gather x1, blocking collectives, on_device(): lax.all_gather(vectors, ROW, axis=0, tiled=True)  37.8 us
  transfers between devices with their start and end apart: 2, of which 1 were waited for; matrix products, arithmetic and copies ran while one was open for 30% of the time, Pallas kernels for 0%

commit v1 on v0

v1 whole, which is shorter than its diff:
```python
import jax
import jax.numpy as jnp
import numpy as np
from jax import lax
from jax.experimental import pallas as pl
from jax.experimental.pallas import tpu as pltpu
from jax.sharding import Mesh
from jax.sharding import PartitionSpec as P

MX = 32
MY = 32
NK = 1024
NB = 16
NG = 1024
NV = 32
NT = NK * NB
NQ = 289
NAMES = ("zh", "zl", "yl", "c", "x", "yh")
SIZES = (4, 2, 2, 2, 4, 4)
A = ("x", "yh", "yl")
B = ("zh", "zl", "c")
NA = 32
NBB = 16
ND = NA * NBB
HALF = NG // 2
LANES = 128

f32 = jnp.float32
bf16 = jnp.bfloat16
HIGH = lax.Precision.HIGHEST


def split_table(x):
    hi = x.astype(bf16)
    lo = (x - hi.astype(np.float64)).astype(bf16)
    return np.concatenate([hi, lo], axis=0)


def cas_tables():
    m = np.arange(32)
    phase = 2.0 * np.pi * ((m[:, None] * m[None, :]) % 32) / 32.0
    cas = np.cos(phase) + np.sin(phase)
    first = np.repeat(cas, 32, axis=1)
    second = np.tile(cas, (1, 32)) / 32.0
    return split_table(first), split_table(second)


def cos_table():
    f = np.arange(17)
    m = np.arange(32)
    weight = np.where((f == 0) | (f == 16), 1.0, 2.0)
    c = weight[:, None] * np.cos(2.0 * np.pi * ((f[:, None] * m[None, :]) % 32) / 32.0)
    return np.einsum("im,jn->ijmn", c, c).reshape(NQ, NK).astype(np.float32)


def iota(shape, axis):
    return lax.broadcasted_iota(jnp.int32, shape, axis)


def block_sum(x):
    x = x + pltpu.roll(x, 32, 1)
    return x + pltpu.roll(x, 64, 1)


def keep_block(x, wanted):
    return jnp.where(iota(x.shape, 1) // 32 == wanted, x, 0.0)


def spread_vectors(vec_ref, wide):
    rows = [
        vec_ref[k : k + 1, v * LANES : (v + 1) * LANES].astype(f32)
        for k in range(2)
        for v in range(4)
    ]
    x8 = jnp.concatenate(rows, axis=0)
    for c in range(4):
        wide[pl.ds(c, 8, stride=4), :] = x8
    x = wide[...]
    return block_sum(keep_block(x, iota(x.shape, 0) % 4))


def energy_column(energy_ref):
    first = jnp.broadcast_to(energy_ref[0:1, :], (NB, NB))
    second = jnp.broadcast_to(energy_ref[1:2, :], (NB, NB))
    e = jnp.concatenate([first, second], axis=0)
    return jnp.sum(
        jnp.where(iota(e.shape, 1) == iota(e.shape, 0) % NB, e, 0.0), axis=1, keepdims=True
    )


def exchange_rows(pe_ref):
    return jnp.concatenate(
        [pe_ref[k, :, g * HALF : (g + 1) * HALF] for g in range(2) for k in range(2)], axis=0
    )


def dot_t(x, y):
    return lax.dot_general(x, y, (((0,), (0,)), ((), ())), preferred_element_type=f32)


def dot_nt(x, y):
    return lax.dot_general(x, y, (((1,), (1,)), ((), ())), preferred_element_type=f32)


def pack_kernel(coords, cond, val, pe, vec, energy, msg, pairs, gram, wide, rows, lines):
    x = spread_vectors(vec, wide)
    for k in range(2):
        cf = cond[k].astype(f32)
        vf = val[k].astype(f32)
        for v in range(4):
            both = vf[v : v + 1, :] * cf
            for g in range(2):
                at = k * 32 + g * 16 + v * 4
                rows[at : at + 4, :] = both[:, g * HALF : (g + 1) * HALF]
    left = rows[...].astype(bf16)
    pairs[...] = left
    xp = jnp.concatenate([x[0:16], x[0:16], x[16:32], x[16:32]], axis=0)
    xp = keep_block(xp, iota(xp.shape, 0) // 16).astype(bf16)
    xd = jnp.concatenate([x, x], axis=0)
    xd = keep_block(xd, iota(xd.shape, 0) // 32).astype(bf16)
    lane = iota((1, LANES), 1)
    place = jnp.zeros((1, LANES), f32)
    for k in range(2):
        for s in range(2):
            place = jnp.where(lane == 64 + 2 * k + s, coords[k, s].astype(f32), place)
    lines[pl.ds(0, ND, stride=2), :] = dot_t(left, xp)
    lines[pl.ds(1, ND, stride=2), :] = dot_t(exchange_rows(pe), xd) + place
    msg[...] = lines[...].astype(bf16)
    gram[...] = lax.dot_general(
        x[:, 0:32],
        energy_column(energy) * x,
        (((0,), (0,)), ((), ())),
        precision=HIGH,
        preferred_element_type=f32,
    )


def spectrum_kernel(where, low, high, cos, lam):
    lane = iota((NQ, LANES), 1)
    out = []
    for ref in (low, high):
        column = jnp.sum(jnp.where(lane == where[1], ref[...], 0.0), axis=1, keepdims=True)
        out.append(jnp.sum(column * cos[...], axis=0, keepdims=True))
    lam[...] = jnp.concatenate(out + [jnp.zeros((6, NK), f32)], axis=0)


def spectral_kernel(where, got, lam, gram, coulomb, first, second, msg, lines, wide):
    lines[...] = got[...].astype(f32)
    proj = lines[pl.ds(0, ND, stride=2), :].astype(bf16)
    rest = lines[pl.ds(1, ND, stride=2), :]
    basis = []
    hat = None
    slot = iota((ND, 64), 1) % 32
    for k in range(2):
        at = [rest[:, 64 + 2 * k + s : 65 + 2 * k + s].astype(jnp.int32) for s in range(2)]
        ones = [jnp.where(slot == p, 1.0, 0.0).astype(bf16) for p in at]
        ta = jnp.dot(ones[0], first[...], preferred_element_type=f32)
        tb = jnp.dot(ones[1], second[...], preferred_element_type=f32)
        t = (ta * tb).astype(bf16)
        basis.append(t)
        part = dot_t(proj, t)[k * 64 : (k + 1) * 64]
        hat = part if hat is None else hat + part
    scale = jnp.concatenate(
        [jnp.broadcast_to(lam[0:1, :], (32, NK)), jnp.broadcast_to(lam[1:2, :], (32, NK))], axis=0
    )
    scaled = (hat * scale).astype(bf16)
    hat = hat.astype(bf16)
    none = jnp.zeros((64, NK), bf16)
    lines[0:ND, :] = dot_nt(basis[0], jnp.concatenate([scaled, none], axis=0)) + dot_nt(
        basis[1], jnp.concatenate([none, scaled], axis=0)
    )
    for a in range(NA):
        msg[a, 0:16, :] = lines[pl.ds(a, NBB, stride=NA), :].astype(bf16)
    direct = dot_nt(hat[0:32], jnp.concatenate([scaled[0:32]] * 4, axis=0)) + dot_nt(
        hat[32:64], jnp.concatenate([scaled[32:64]] * 4, axis=0)
    )
    lane = iota((1, LANES), 1)
    dens = jnp.sum(rest, axis=0, keepdims=True)
    index = iota((8, LANES), 0) * LANES + iota((8, LANES), 1)
    outer = jnp.zeros((32, LANES), f32)
    cd = jnp.zeros((1, LANES), f32)
    for g in range(2):
        factor = jnp.sum(jnp.where(index == where[0] + g * HALF, coulomb[...], 0.0), keepdims=True)
        own = jnp.where(lane // 32 == g, dens, 0.0)
        row = block_sum(own)
        column = jnp.sum(
            jnp.where(iota((32, LANES), 0) == iota((32, LANES), 1), row, 0.0), axis=1, keepdims=True
        )
        outer = outer + column * (factor * row)
        cd = cd + factor * own
    alpha = (gram[...] + (2.0 / NT) * outer - direct / NK) / NT
    wide[...] = keep_block(alpha, iota((32, LANES), 0) % 4)
    packed = wide[pl.ds(0, 8, stride=4), :]
    for c in range(1, 4):
        packed = packed + wide[pl.ds(c, 8, stride=4), :]
    tail = jnp.concatenate([packed, jnp.broadcast_to(cd, (8, LANES))], axis=0).astype(bf16)
    msg[:, 16:32, :] = jnp.broadcast_to(tail[None], (NA, 16, LANES))


def relay_kernel(got, msg, lines):
    for a in range(NA):
        lines[a * 32 : (a + 1) * 32, :] = got[a].astype(f32)
    alpha = lines[16:24, :]
    for a in range(1, NA):
        alpha = alpha + lines[a * 32 + 16 : a * 32 + 24, :]
    hi = alpha.astype(bf16)
    lo = (alpha - hi.astype(f32)).astype(bf16)
    cd = lines[pl.ds(24, NA, stride=32), :].astype(bf16)
    tail = jnp.concatenate([cd, hi, lo], axis=0)
    for s in range(NBB):
        msg[s, 0:32, :] = lines[pl.ds(s, NA, stride=32), :].astype(bf16)
        msg[s, 32:80, :] = tail


def finish_kernel(got, pairs, pe, vec, energy, out, alpha_out, wide, rows):
    x = spread_vectors(vec, wide)
    potential = got[:, 0:32, :].reshape(ND, LANES)
    field = got[:, 32:64, :].reshape(ND, LANES)
    direct = jnp.dot(pairs[...], potential, preferred_element_type=f32)
    direct = block_sum(keep_block(direct, iota(direct.shape, 0) // 16))
    direct = jnp.concatenate([direct[0:16] + direct[16:32], direct[32:48] + direct[48:64]], axis=0)
    exchange = jnp.dot(exchange_rows(pe), field, preferred_element_type=f32)
    exchange = block_sum(keep_block(exchange, iota(exchange.shape, 0) // 32))
    exchange = exchange[0:32] + exchange[32:64]
    applied = energy_column(energy) * x + (2.0 / NT) * exchange - direct / NK
    alpha = jnp.zeros((16, LANES), f32)
    for b in range(NBB):
        alpha = alpha + got[b, 64:80, :].astype(f32)
    alpha = alpha[0:8] + alpha[8:16]
    for c in range(4):
        wide[pl.ds(c, 8, stride=4), :] = alpha
    full = wide[...]
    full = block_sum(keep_block(full, iota(full.shape, 0) % 4))
    alpha_out[...] = full[:, 0:32]
    shift = jnp.dot(x[:, 0:32], full, precision=HIGH, preferred_element_type=f32)
    rows[...] = keep_block(applied - shift, iota((32, LANES), 0) % 4)
    packed = rows[pl.ds(0, 8, stride=4), :]
    for c in range(1, 4):
        packed = packed + rows[pl.ds(c, 8, stride=4), :]
    for k in range(2):
        for v in range(4):
            out[k : k + 1, v * LANES : (v + 1) * LANES] = packed[k * 4 + v : k * 4 + v + 1, :]


def vmem():
    return pl.BlockSpec(memory_space=pltpu.VMEM)


def smem():
    return pl.BlockSpec(memory_space=pltpu.SMEM)


def sds(shape, dtype):
    return jax.ShapeDtypeStruct(shape, dtype)


def on_device(pair_exchange, conduction, valence, coulomb, screening, energies, vectors, k_coords):
    mine = lax.axis_index(B) * NA + lax.axis_index(A)
    msg, pairs, gram = pl.pallas_call(
        pack_kernel,
        out_shape=(sds((2 * ND, LANES), bf16), sds((64, HALF), bf16), sds((32, LANES), f32)),
        in_specs=[smem()] + [vmem()] * 5,
        out_specs=(vmem(),) * 3,
        scratch_shapes=[
            pltpu.VMEM((32, LANES), f32),
            pltpu.VMEM((64, HALF), f32),
            pltpu.VMEM((2 * ND, LANES), f32),
        ],
        name="pack",
    )(k_coords, conduction, valence, pair_exchange, vectors, energies)
    got = lax.all_to_all(msg.reshape(ND, 2, LANES), B + A, 0, 0, tiled=True)
    place = jnp.stack([mine // LANES, mine % LANES]).astype(jnp.int32)
    lam = pl.pallas_call(
        spectrum_kernel,
        out_shape=sds((8, NK), f32),
        grid_spec=pltpu.PrefetchScalarGridSpec(
            num_scalar_prefetch=1,
            grid=(1,),
            in_specs=[
                pl.BlockSpec((NQ, LANES), lambda i, w: (0, w[0])),
                pl.BlockSpec((NQ, LANES), lambda i, w: (0, w[0] + HALF // LANES)),
                pl.BlockSpec((NQ, NK), lambda i, w: (0, 0)),
            ],
            out_specs=pl.BlockSpec((8, NK), lambda i, w: (0, 0)),
        ),
        name="spectrum",
    )(place, screening, screening, cos_table())
    first, second = cas_tables()
    out = pl.pallas_call(
        spectral_kernel,
        out_shape=sds((NA, 32, LANES), bf16),
        in_specs=[smem()] + [vmem()] * 6,
        out_specs=vmem(),
        scratch_shapes=[pltpu.VMEM((2 * ND, LANES), f32), pltpu.VMEM((32, LANES), f32)],
        name="spectral",
    )(
        mine.reshape(1).astype(jnp.int32),
        got.reshape(2 * ND, LANES),
        lam,
        gram,
        coulomb.reshape(8, LANES),
        first,
        second,
    )
    got = lax.all_to_all(out, A, 0, 0, tiled=True)
    out = pl.pallas_call(
        relay_kernel,
        out_shape=sds((NBB, 80, LANES), bf16),
        in_specs=[vmem()],
        out_specs=vmem(),
        scratch_shapes=[pltpu.VMEM((NA * 32, LANES), f32)],
        name="relay",
    )(got)
    got = lax.all_to_all(out, B, 0, 0, tiled=True)
    return pl.pallas_call(
        finish_kernel,
        out_shape=(sds((2, NB * NV), f32), sds((NV, NV), f32)),
        in_specs=[vmem()] * 5,
        out_specs=(vmem(), vmem()),
        scratch_shapes=[pltpu.VMEM((32, LANES), f32), pltpu.VMEM((32, LANES), f32)],
        name="finish",
    )(got, pairs, pair_exchange, vectors, energies)


def solution(mesh):
    split = Mesh(mesh.devices.reshape(SIZES), NAMES)
    return jax.shard_map(
        on_device,
        mesh=split,
        in_specs=(
            P(NAMES, None, None),
            P(NAMES, None, None),
            P(NAMES, None, None),
            P(),
            P(),
            P(NAMES, None),
            P(NAMES, None),
            P(NAMES, None),
        ),
        out_specs=(P(NAMES, None), P()),
        check_vma=False,
    )
```

time: 630 us -> 86.8 us (0.14); the launches traced: 623 us -> 86.4 us
  blocking collectives: 337 us -> 35.2 us
  local copies, waits for them, and re-layouts: 115 us -> 0.69 us
  matrix products: 70.7 us -> 0 us
  waiting for transfers between devices: 79.5 us -> 13.2 us
  starting transfers between devices: 0.08 us -> 22.1 us
  between operations: 15.6 us -> 0.67 us
  Pallas kernels: 0 us -> 13.8 us
    all_gather x7 -> x0, blocking collectives: 267 us -> none  [the longest x1 42.1 us: on_device(): lax.all_gather(k_coords, ROW, axis=0, tiled=True)]
    reduce_scatter x1 -> x0, waiting for transfers between devices: 79.4 us -> none  [on_device(): lax.psum_scatter(forward.reshape(col_count, local_count, band_count, vect...]
    psum x5 -> x0, blocking collectives: 70.7 us -> none  [over_axes(): return functools.reduce(lax.psum, axes, x)]
    dot_general x28 -> x0, matrix products: 70.7 us -> none  [the longest x8 45.6 us: square_sweep(): jnp.einsum('ijg,jng->ing', coupling, col_proj, precision=highest)]
    gather x16 -> x0, local copies, waits for them, and re-layouts: 66.3 us -> none  [square_sweep(): jnp.take(lax.dynamic_slice_in_dim(screening, anchor, block_size, 1), indi...]
    all_to_all x0 -> x2, blocking collectives: none -> 35.2 us  [the longest x1 20.9 us: on_device(): got = lax.all_to_all(out, B, 0, 0, tiled=True)]
    dot_general x8 -> x0, local copies, waits for them, and re-layouts: 23.2 us -> none  [square_sweep(): jnp.einsum('ktg,ktn->kng', col_block, col_moving, preferred_element_type=...]
    all_to_all x0 -> x1, starting transfers between devices: none -> 22.1 us  [on_device(): got = lax.all_to_all(msg.reshape(ND, 2, LANES), B + A, 0, 0, tiled=True)]
  transfers between devices with their start and end apart: 2 -> 1, of which waited for: 1 -> 1; matrix products, arithmetic and copies ran while one was open for 30% -> 1% of each run, Pallas kernels for 0% -> 3%
where the time goes in v1:
time: 86.8 us; the launch traced here: 86.4 us
  blocking collectives  35.2 us (41%)
  starting transfers between devices  22.1 us (25%)
  Pallas kernels  13.8 us (16%)
  waiting for transfers between devices  13.2 us (15%)
    all_to_all x1, starting transfers between devices, on_device(): got = lax.all_to_all(msg.reshape(ND, 2, LANES), B + A, 0, 0, tiled=True)  22.1 us
    all_to_all x1, blocking collectives, on_device(): got = lax.all_to_all(out, B, 0, 0, tiled=True)  20.9 us
    all_to_all x1, blocking collectives, on_device(): got = lax.all_to_all(out, A, 0, 0, tiled=True)  14.3 us
    all_to_all x1, waiting for transfers between devices, on_device(): got = lax.all_to_all(msg.reshape(ND, 2, LANES), B + A, 0, 0, tiled=True)  13.2 us
    pallas_call x1, Pallas kernels, on_device(): pl.pallas_call(spectral_kernel, out_shape=sds((NA, 32, LANES), bf16), in_...  4.94 us
    pallas_call x1, Pallas kernels, on_device(): pl.pallas_call(spectrum_kernel, out_shape=sds((8, NK), f32), grid_spec=pl...  2.97 us
    pallas_call x1, Pallas kernels, on_device(): pl.pallas_call(pack_kernel, out_shape=(sds((2 * ND, LANES), bf16), sds((6...  2.06 us
    pallas_call x1, Pallas kernels, on_device(): pl.pallas_call(finish_kernel, out_shape=(sds((2, NB * NV), f32), sds((NV,...  2 us
  transfers between devices with their start and end apart: 1, of which 1 were waited for; matrix products, arithmetic and copies ran while one was open for 1% of the time, Pallas kernels for 3%

profile of v1, /device:TPU:1, one launch (start us, length us, event | category | flops | bytes accessed | tf_op | source)
XLA Modules:
  0.0 86.4 jit_solution(7069058275785028998)
XLA Ops:
  0.6 2.1 %pack.1 = (bf16[1024,128]{1,0:T(8,128)(2,1)}, bf16[64,512]{1,0:T(8,128)(2,1)}, f32[32,128]{1,0:T(8,128)}) custom-call(s32[2,2]{1,0:T(2,128)} %coords.1, bf16[2,4,1024]{2,1,0:T(4,128)(2,1)} %cond.1, bf16[2,4,1024]{2,1,0:T(4,128)(2,1)} %val.1, bf16[2,16,1024]{2,1,0:T(8,128)(2,1)} %pe.3, bf16[2,512]{1,0:T(2,128)(2,1)} %vec.3, f32[2,16]{1,0:T(2,128)} %energy.3), custom_call_target="tpu_custom_call" | custom-call | tf_op jit(solution)/shard_map/pack/pallas_call | solution.py:259
  2.7 22.1 %all-to-all-start = ((bf16[512,2,128]{2,1,0:T(2,128)(2,1)}), bf16[512,2,128]{2,1,0:T(2,128)(2,1)S(1)}, u32[]{:S(2)}, u32[]{:S(2)}) async-start(bf16[512,2,128]{2,1,0:T(2,128)(2,1)} %bitcast.7), calls=%async_computation | async-start | bytes 524288 | tf_op jit(solution)/shard_map/all_to_all | solution.py:271
  24.9 0.7 pad_add_fusion.where
  25.5 3.0 %spectrum.1.lam = f32[8,1024]{1,0:T(8,128)} custom-call(s32[2]{0:T(128)} %pad_add_fusion.where, f32[289,1024]{1,0:T(8,128)} %high.1, f32[289,1024]{1,0:T(8,128)} %high.1, f32[289,1024]{1,0:T(8,128)} %constant.65.clone.cos), custom_call_target="tpu_custom_call" | custom-call | tf_op jit(solution)/shard_map/spectrum/pallas_call | solution.py:273
  28.5 13.2 %all-to-all-done = bf16[512,2,128]{2,1,0:T(2,128)(2,1)S(1)} async-done(((bf16[512,2,128]{2,1,0:T(2,128)(2,1)}), bf16[512,2,128]{2,1,0:T(2,128)(2,1)S(1)}, u32[]{:S(2)}, u32[]{:S(2)}) %all-to-all-start) | async-done | bytes 262176 | tf_op jit(solution)/shard_map/all_to_all | solution.py:271
  41.7 0.0 copy-start
  41.7 0.7 copy-done
  42.4 4.9 %spectral.1 = bf16[32,32,128]{2,1,0:T(8,128)(2,1)} custom-call(s32[1]{0:T(128)} %bitcast.where, bf16[1024,128]{1,0:T(8,128)(2,1)} %bitcast.6, f32[8,1024]{1,0:T(8,128)} %spectrum.1.lam, f32[32,128]{1,0:T(8,128)} %get-tuple-element.6.gram, f32[8,128]{1,0:T(8,128)} %bitcast.8, bf16[64,1024]{1,0:T(8,128)(2,1)} %constant.66.clone.first, ...), custom_call_target="tpu_custom_call" | custom-call | tf_op jit(solution)/shard_map/spectral/pallas_call | solution.py:289
  47.3 14.3 %all_to_all.15.got = bf16[32,32,128]{2,1,0:T(8,128)(2,1)} all-to-all(bf16[32,32,128]{2,1,0:T(8,128)(2,1)} %spectral.1), channel_id=1, replica_groups=mesh['zh'=4,'zl'=2,'yl'=2,'c'=2,'x'=4,'yh'=4] {'x','yh','yl'}, dimensions={0} | all-to-all | bytes 524288 | tf_op jit(solution)/shard_map/all_to_all | solution.py:305
  61.6 1.9 %relay.1 = bf16[16,80,128]{2,1,0:T(8,128)(2,1)} custom-call(bf16[32,32,128]{2,1,0:T(8,128)(2,1)} %all_to_all.15.got), custom_call_target="tpu_custom_call" | custom-call | tf_op jit(solution)/shard_map/relay/pallas_call | solution.py:306
  63.4 20.9 %all_to_all.16.got = bf16[16,80,128]{2,1,0:T(8,128)(2,1)} all-to-all(bf16[16,80,128]{2,1,0:T(8,128)(2,1)} %relay.1), channel_id=1, replica_groups=mesh['zh'=4,'zl'=2,'yl'=2,'c'=2,'x'=4,'yh'=4] {'zh','zl','c'}, dimensions={0} | all-to-all | bytes 655360 | tf_op jit(solution)/shard_map/all_to_all | solution.py:314
  84.4 2.0 %finish.1 = (f32[2,512]{1,0:T(2,128)}, f32[32,32]{1,0:T(8,128)}) custom-call(bf16[16,80,128]{2,1,0:T(8,128)(2,1)} %all_to_all.16.got, bf16[64,512]{1,0:T(8,128)(2,1)} %get-tuple-element.7.pairs, bf16[2,16,1024]{2,1,0:T(8,128)(2,1)} %pe.3, bf16[2,512]{1,0:T(2,128)(2,1)} %vec.3, f32[2,16]{1,0:T(2,128)} %energy.3), custom_call_target="tpu_custom_call" | custom-call | tf_op jit(solution)/shard_map/finish/pallas_call | solution.py:315
Async XLA Ops:
  2.7 39.0 %all-to-all-start = ((bf16[512,2,128]{2,1,0:T(2,128)(2,1)}), bf16[512,2,128]{2,1,0:T(2,128)(2,1)S(1)}, u32[]{:S(2)}, u32[]{:S(2)}) async-start(bf16[512,2,128]{2,1,0:T(2,128)(2,1)} %bitcast.7), calls=%async_computation | async-start | bytes 524288 | tf_op jit(solution)/shard_map/all_to_all | solution.py:271
  41.7 0.7 copy-start

commit v2 on v1

--- a/solution.py
+++ b/solution.py
@@ -23,6 +23,7 @@
 NBB = 16
 ND = NA * NBB
 HALF = NG // 2
+ROWS = 26
 LANES = 128
 
 f32 = jnp.float32
@@ -102,7 +103,9 @@
     return lax.dot_general(x, y, (((1,), (1,)), ((), ())), preferred_element_type=f32)
 
 
-def pack_kernel(coords, cond, val, pe, vec, energy, msg, pairs, gram, wide, rows, lines):
+def pack_kernel(
+    mine, coords, cond, val, pe, vec, energy, low, high, cos, msg, pairs, gram, lam, wide, rows, lines
+):
     x = spread_vectors(vec, wide)
     for k in range(2):
         cf = cond[k].astype(f32)
@@ -133,13 +136,10 @@
         precision=HIGH,
         preferred_element_type=f32,
     )
-
-
-def spectrum_kernel(where, low, high, cos, lam):
-    lane = iota((NQ, LANES), 1)
+    own = iota((NQ, LANES), 1) == mine[0] % LANES
     out = []
     for ref in (low, high):
-        column = jnp.sum(jnp.where(lane == where[1], ref[...], 0.0), axis=1, keepdims=True)
+        column = jnp.sum(jnp.where(own, ref[...], 0.0), axis=1, keepdims=True)
         out.append(jnp.sum(column * cos[...], axis=0, keepdims=True))
     lam[...] = jnp.concatenate(out + [jnp.zeros((6, NK), f32)], axis=0)
 
@@ -156,21 +156,28 @@
         ones = [jnp.where(slot == p, 1.0, 0.0).astype(bf16) for p in at]
         ta = jnp.dot(ones[0], first[...], preferred_element_type=f32)
         tb = jnp.dot(ones[1], second[...], preferred_element_type=f32)
-        t = (ta * tb).astype(bf16)
-        basis.append(t)
-        part = dot_t(proj, t)[k * 64 : (k + 1) * 64]
+        exact = ta * tb
+        hi = exact.astype(bf16)
+        lo = (exact - hi.astype(f32)).astype(bf16)
+        basis.append((hi, lo))
+        part = (dot_t(proj, hi) + dot_t(proj, lo))[k * 64 : (k + 1) * 64]
         hat = part if hat is None else hat + part
     scale = jnp.concatenate(
         [jnp.broadcast_to(lam[0:1, :], (32, NK)), jnp.broadcast_to(lam[1:2, :], (32, NK))], axis=0
     )
-    scaled = (hat * scale).astype(bf16)
+    exact = hat * scale
+    scaled = exact.astype(bf16)
+    finer = (exact - scaled.astype(f32)).astype(bf16)
     hat = hat.astype(bf16)
-    none = jnp.zeros((64, NK), bf16)
-    lines[0:ND, :] = dot_nt(basis[0], jnp.concatenate([scaled, none], axis=0)) + dot_nt(
-        basis[1], jnp.concatenate([none, scaled], axis=0)
-    )
-    for a in range(NA):
-        msg[a, 0:16, :] = lines[pl.ds(a, NBB, stride=NA), :].astype(bf16)
+    both = jnp.concatenate([scaled, finer], axis=0)
+    side = iota((ND, LANES), 1) // 64
+    back = []
+    for hi, lo in basis:
+        r = dot_nt(hi, both)
+        back.append(r + pltpu.roll(r, 64, 1) + dot_nt(lo, jnp.concatenate([scaled] * 2, axis=0)))
+    back = jnp.where(side == 0, back[0], back[1])
+    for b in range(NBB):
+        lines[pl.ds(b, NA, stride=ROWS), :] = back[b * NA : (b + 1) * NA]
     direct = dot_nt(hat[0:32], jnp.concatenate([scaled[0:32]] * 4, axis=0)) + dot_nt(
         hat[32:64], jnp.concatenate([scaled[32:64]] * 4, axis=0)
     )
@@ -193,29 +200,36 @@
     packed = wide[pl.ds(0, 8, stride=4), :]
     for c in range(1, 4):
         packed = packed + wide[pl.ds(c, 8, stride=4), :]
-    tail = jnp.concatenate([packed, jnp.broadcast_to(cd, (8, LANES))], axis=0).astype(bf16)
-    msg[:, 16:32, :] = jnp.broadcast_to(tail[None], (NA, 16, LANES))
+    tail = jnp.concatenate([packed, cd, jnp.zeros((1, LANES), f32)], axis=0)
+    for r in range(ROWS - NBB):
+        lines[pl.ds(NBB + r, NA, stride=ROWS), :] = jnp.broadcast_to(tail[r : r + 1], (NA, LANES))
+    msg[...] = lines[0 : NA * ROWS, :].astype(bf16)
 
 
 def relay_kernel(got, msg, lines):
-    for a in range(NA):
-        lines[a * 32 : (a + 1) * 32, :] = got[a].astype(f32)
-    alpha = lines[16:24, :]
-    for a in range(1, NA):
-        alpha = alpha + lines[a * 32 + 16 : a * 32 + 24, :]
-    hi = alpha.astype(bf16)
-    lo = (alpha - hi.astype(f32)).astype(bf16)
-    cd = lines[pl.ds(24, NA, stride=32), :].astype(bf16)
-    tail = jnp.concatenate([cd, hi, lo], axis=0)
-    for s in range(NBB):
-        msg[s, 0:32, :] = lines[pl.ds(s, NA, stride=32), :].astype(bf16)
-        msg[s, 32:80, :] = tail
+    lines[...] = got[...].astype(f32)
+    alpha = []
+    for r in range(8):
+        part = lines[pl.ds(NBB + r, NA, stride=ROWS), :]
+        alpha.append(jnp.sum(part, axis=0, keepdims=True))
+    alpha = jnp.concatenate(alpha, axis=0)
+    hi = alpha.astype(bf16).astype(f32)
+    cd = lines[pl.ds(NBB + 8, NA, stride=ROWS), :]
+    cd = cd[0:16] + pltpu.roll(cd[16:32], 64, 1)
+    tail = jnp.concatenate([cd, hi, alpha - hi], axis=0).astype(bf16)
+    for b in range(NBB):
+        msg[b, 0:32, :] = lines[pl.ds(b, NA, stride=ROWS), :].astype(bf16)
+        msg[b, 32:64, :] = tail
 
 
 def finish_kernel(got, pairs, pe, vec, energy, out, alpha_out, wide, rows):
     x = spread_vectors(vec, wide)
     potential = got[:, 0:32, :].reshape(ND, LANES)
-    field = got[:, 32:64, :].reshape(ND, LANES)
+    field = []
+    for b in range(NBB):
+        part = got[b, 32:48, :].astype(f32)
+        field += [part, pltpu.roll(part, 64, 1)]
+    field = jnp.concatenate(field, axis=0).astype(bf16)
     direct = jnp.dot(pairs[...], potential, preferred_element_type=f32)
     direct = block_sum(keep_block(direct, iota(direct.shape, 0) // 16))
     direct = jnp.concatenate([direct[0:16] + direct[16:32], direct[32:48] + direct[48:64]], axis=0)
@@ -225,7 +239,7 @@
     applied = energy_column(energy) * x + (2.0 / NT) * exchange - direct / NK
     alpha = jnp.zeros((16, LANES), f32)
     for b in range(NBB):
-        alpha = alpha + got[b, 64:80, :].astype(f32)
+        alpha = alpha + got[b, 48:64, :].astype(f32)
     alpha = alpha[0:8] + alpha[8:16]
     for c in range(4):
         wide[pl.ds(c, 8, stride=4), :] = alpha
@@ -250,51 +264,77 @@
     return pl.BlockSpec(memory_space=pltpu.SMEM)
 
 
+def room(mib):
+    return pltpu.CompilerParams(vmem_limit_bytes=mib << 20)
+
+
 def sds(shape, dtype):
     return jax.ShapeDtypeStruct(shape, dtype)
 
 
 def on_device(pair_exchange, conduction, valence, coulomb, screening, energies, vectors, k_coords):
-    mine = lax.axis_index(B) * NA + lax.axis_index(A)
-    msg, pairs, gram = pl.pallas_call(
+    mine = (lax.axis_index(B) * NA + lax.axis_index(A)).reshape(1).astype(jnp.int32)
+    fixed2 = lambda i, *w: (0, 0)
+    fixed3 = lambda i, *w: (0, 0, 0)
+    msg, pairs, gram, lam = pl.pallas_call(
         pack_kernel,
-        out_shape=(sds((2 * ND, LANES), bf16), sds((64, HALF), bf16), sds((32, LANES), f32)),
-        in_specs=[smem()] + [vmem()] * 5,
-        out_specs=(vmem(),) * 3,
-        scratch_shapes=[
-            pltpu.VMEM((32, LANES), f32),
-            pltpu.VMEM((64, HALF), f32),
-            pltpu.VMEM((2 * ND, LANES), f32),
-        ],
-        name="pack",
-    )(k_coords, conduction, valence, pair_exchange, vectors, energies)
-    got = lax.all_to_all(msg.reshape(ND, 2, LANES), B + A, 0, 0, tiled=True)
-    place = jnp.stack([mine // LANES, mine % LANES]).astype(jnp.int32)
-    lam = pl.pallas_call(
-        spectrum_kernel,
-        out_shape=sds((8, NK), f32),
+        out_shape=(
+            sds((2 * ND, LANES), bf16),
+            sds((64, HALF), bf16),
+            sds((32, LANES), f32),
+            sds((8, NK), f32),
+        ),
         grid_spec=pltpu.PrefetchScalarGridSpec(
-            num_scalar_prefetch=1,
+            num_scalar_prefetch=2,
             grid=(1,),
             in_specs=[
-                pl.BlockSpec((NQ, LANES), lambda i, w: (0, w[0])),
-                pl.BlockSpec((NQ, LANES), lambda i, w: (0, w[0] + HALF // LANES)),
-                pl.BlockSpec((NQ, NK), lambda i, w: (0, 0)),
+                pl.BlockSpec(conduction.shape, fixed3),
+                pl.BlockSpec(valence.shape, fixed3),
+                pl.BlockSpec(pair_exchange.shape, fixed3),
+                pl.BlockSpec(vectors.shape, fixed2),
+                pl.BlockSpec(energies.shape, fixed2),
+                pl.BlockSpec((NQ, LANES), lambda i, w, c: (0, w[0] // LANES)),
+                pl.BlockSpec((NQ, LANES), lambda i, w, c: (0, w[0] // LANES + HALF // LANES)),
+                pl.BlockSpec((NQ, NK), fixed2),
             ],
-            out_specs=pl.BlockSpec((8, NK), lambda i, w: (0, 0)),
+            out_specs=[
+                pl.BlockSpec((2 * ND, LANES), fixed2),
+                pl.BlockSpec((64, HALF), fixed2),
+                pl.BlockSpec((32, LANES), fixed2),
+                pl.BlockSpec((8, NK), fixed2),
+            ],
+            scratch_shapes=[
+                pltpu.VMEM((32, LANES), f32),
+                pltpu.VMEM((64, HALF), f32),
+                pltpu.VMEM((2 * ND, LANES), f32),
+            ],
         ),
-        name="spectrum",
-    )(place, screening, screening, cos_table())
+        compiler_params=room(12),
+        name="pack",
+    )(
+        mine,
+        k_coords,
+        conduction,
+        valence,
+        pair_exchange,
+        vectors,
+        energies,
+        screening,
+        screening,
+        cos_table(),
+    )
+    got = lax.all_to_all(msg.reshape(ND, 2, LANES), B + A, 0, 0, tiled=True)
     first, second = cas_tables()
     out = pl.pallas_call(
         spectral_kernel,
-        out_shape=sds((NA, 32, LANES), bf16),
+        out_shape=sds((NA * ROWS, LANES), bf16),
         in_specs=[smem()] + [vmem()] * 6,
         out_specs=vmem(),
         scratch_shapes=[pltpu.VMEM((2 * ND, LANES), f32), pltpu.VMEM((32, LANES), f32)],
+        compiler_params=room(28),
         name="spectral",
     )(
-        mine.reshape(1).astype(jnp.int32),
+        mine,
         got.reshape(2 * ND, LANES),
         lam,
         gram,
@@ -302,15 +342,16 @@
         first,
         second,
     )
-    got = lax.all_to_all(out, A, 0, 0, tiled=True)
+    got = lax.all_to_all(out.reshape(NA, ROWS // 2, 2, LANES), A, 0, 0, tiled=True)
     out = pl.pallas_call(
         relay_kernel,
-        out_shape=sds((NBB, 80, LANES), bf16),
+        out_shape=sds((NBB, 64, LANES), bf16),
         in_specs=[vmem()],
         out_specs=vmem(),
-        scratch_shapes=[pltpu.VMEM((NA * 32, LANES), f32)],
+        scratch_shapes=[pltpu.VMEM((NA * ROWS, LANES), f32)],
+        compiler_params=room(8),
         name="relay",
-    )(got)
+    )(got.reshape(NA * ROWS, LANES))
     got = lax.all_to_all(out, B, 0, 0, tiled=True)
     return pl.pallas_call(
         finish_kernel,
@@ -318,6 +359,7 @@
         in_specs=[vmem()] * 5,
         out_specs=(vmem(), vmem()),
         scratch_shapes=[pltpu.VMEM((32, LANES), f32), pltpu.VMEM((32, LANES), f32)],
+        compiler_params=room(8),
         name="finish",
     )(got, pairs, pair_exchange, vectors, energies)
 

time: 86.8 us -> 83.1 us (0.957)
  blocking collectives: 35.2 us -> 69.5 us
  starting transfers between devices: 22.1 us -> 0 us
  waiting for transfers between devices: 13.2 us -> 0 us
  Pallas kernels: 13.8 us -> 5.56 us
  local copies, waits for them, and re-layouts: 0.69 us -> 6.89 us
    all_to_all x1 -> x2, blocking collectives: 14.3 us -> 51.6 us  [the longest x1 38.8 us: on_device(): got = lax.all_to_all(msg.reshape(ND, 2, LANES), B + A, 0, 0, tiled=True)]
    all_to_all x1 -> x0, starting transfers between devices: 22.1 us -> none  [on_device(): got = lax.all_to_all(msg.reshape(ND, 2, LANES), B + A, 0, 0, tiled=True)]
    all_to_all x1 -> x0, waiting for transfers between devices: 13.2 us -> none  [on_device(): got = lax.all_to_all(msg.reshape(ND, 2, LANES), B + A, 0, 0, tiled=True)]
    pallas_call x3 -> x2, Pallas kernels: 9.76 us -> 3.43 us  [the longest x1 3.35 us: on_device(): pl.pallas_call(spectral_kernel, out_shape=sds((NA * ROWS, LANES), bf16),...]
    unnamed x2 -> x28, local copies, waits for them, and re-layouts: 0.69 us -> 6.89 us
    all_to_all x1, blocking collectives: 20.9 us -> 17.9 us  [on_device(): got = lax.all_to_all(out, B, 0, 0, tiled=True)]
    pallas_call x1, Pallas kernels: 2 us -> 1 us  [on_device(): pl.pallas_call(finish_kernel, out_shape=(sds((2, NB * NV), f32), sds((NV,...]
    pallas_call x1, Pallas kernels: 2.06 us -> 1.12 us  [on_device(): pl.pallas_call(pack_kernel, out_shape=(sds((2 * ND, LANES), bf16), sds((6...]
  transfers between devices with their start and end apart: 1 -> 0, of which waited for: 1 -> 0; matrix products, arithmetic and copies ran while one was open for 1% -> 0% of each run, Pallas kernels for 3% -> 0%
where the time goes in v2:
time: 83.1 us; the launch traced here: 82.6 us
  blocking collectives  69.5 us (84%)
  local copies, waits for them, and re-layouts  6.89 us (8%)
  Pallas kernels  5.56 us (7%)
    all_to_all x1, blocking collectives, on_device(): got = lax.all_to_all(msg.reshape(ND, 2, LANES), B + A, 0, 0, tiled=True)  38.8 us
    all_to_all x1, blocking collectives, on_device(): got = lax.all_to_all(out, B, 0, 0, tiled=True)  17.9 us
    all_to_all x1, blocking collectives, on_device(): lax.all_to_all(out.reshape(NA, ROWS // 2, 2, LANES), A, 0, 0, tiled=True)  12.7 us
    unnamed x28, local copies, waits for them, and re-layouts  6.89 us
    pallas_call x1, Pallas kernels, on_device(): pl.pallas_call(spectral_kernel, out_shape=sds((NA * ROWS, LANES), bf16),...  3.35 us

profile of v2, /device:TPU:1, one launch (start us, length us, event | category | flops | bytes accessed | tf_op | source)
XLA Modules:
  0.0 82.6 jit_solution(18208882198016276170)
XLA Ops:
  0.6 0.0 copy-start
  0.7 1.3 %copy-done = f32[289,1024]{1,0:T(8,128)S(1)} copy-done((f32[289,1024]{1,0:T(8,128)S(1)}, f32[289,1024]{1,0:T(8,128)}, u32[]{:S(2)}) %copy-start) | copy-done | bytes 1183768
  1.9 0.0 copy-start.1
  1.9 1.3 %copy-done.1 = f32[289,1024]{1,0:T(8,128)S(1)} copy-done((f32[289,1024]{1,0:T(8,128)S(1)}, f32[289,1024]{1,0:T(8,128)}, u32[]{:S(2)}) %copy-start.1) | copy-done | bytes 1183768
  3.2 0.0 copy-start.2
  3.2 0.8 %copy-done.2 = bf16[2,16,1024]{2,1,0:T(8,128)(2,1)S(1)} copy-done((bf16[2,16,1024]{2,1,0:T(8,128)(2,1)S(1)}, bf16[2,16,1024]{2,1,0:T(8,128)(2,1)}, u32[]{:S(2)}) %copy-start.2) | copy-done | bytes 65560
  4.1 0.0 copy-start.6
  4.1 0.7 copy-done.6
  4.8 0.0 copy-start.7
  4.8 0.7 copy-done.7
  5.5 0.0 copy-start.8
  5.5 0.7 copy-done.8
  6.2 0.0 copy-start.11
  6.2 0.7 copy-done.11
  6.8 0.0 copy-start.13
  6.9 0.7 copy-done.13
  7.5 0.0 copy-start.4
  7.5 0.0 copy-start.5
  7.5 0.0 copy-start.10
  7.5 1.1 %pack.1 = (bf16[1024,128]{1,0:T(8,128)(2,1)S(1)}, bf16[64,512]{1,0:T(8,128)(2,1)S(1)}, f32[32,128]{1,0:T(8,128)S(1)}, f32[8,1024]{1,0:T(8,128)S(1)}) custom-call(s32[1]{0:T(128)} %bitcast.mine.where, s32[2,2]{1,0:T(2,128)S(1)} %copy-done.13, bf16[2,4,1024]{2,1,0:T(4,128)(2,1)S(1)} %copy-done.6, bf16[2,4,1024]{2,1,0:T(4,128)(2,1)S(1)} %copy-done.7, ...), custom_call_target="tpu_custom_call" | custom-call | tf_op jit(solution)/shard_map/pack/pallas_call | solution.py:279
  8.7 38.8 %all_to_all.15 = bf16[512,2,128]{2,1,0:T(2,128)(2,1)S(1)} all-to-all(bf16[512,2,128]{2,1,0:T(2,128)(2,1)S(1)} %bitcast.9), channel_id=1, replica_groups=mesh['zh'=4,'zl'=2,'yl'=2,'c'=2,'x'=4,'yh'=4] {'zh','zl','c','x','yh','yl'}, dimensions={0} | all-to-all | bytes 524288 | tf_op jit(solution)/shard_map/all_to_all | solution.py:326
  47.5 0.0 copy-start.3
  47.5 0.0 copy-start.9
  47.5 0.0 copy-start.12
  47.5 0.0 copy-done.4
  47.5 0.0 copy-done.5
  47.5 0.0 copy-done.10
  47.5 3.3 %spectral.1 = bf16[832,128]{1,0:T(8,128)(2,1)S(1)} custom-call(s32[1]{0:T(128)} %bitcast.mine.where, bf16[1024,128]{1,0:T(8,128)(2,1)S(1)} %bitcast.6, f32[8,1024]{1,0:T(8,128)S(1)} %get-tuple-element.7.lam, f32[32,128]{1,0:T(8,128)S(1)} %get-tuple-element.8.gram, f32[8,128]{1,0:T(8,128)S(1)} %bitcast.10, bf16[64,1024]{1,0:T(8,128)(2,1)S(1)} %copy-done.5, ...), custom_call_target="tpu_custom_call" | custom-call | tf_op jit(solution)/shard_map/spectral/pallas_call | solution.py:328
  50.9 12.7 %all_to_all.16 = bf16[32,13,2,128]{3,2,1,0:T(2,128)(2,1)S(1)} all-to-all(bf16[32,13,2,128]{3,2,1,0:T(2,128)(2,1)S(1)} %bitcast.7), channel_id=1, replica_groups=mesh['zh'=4,'zl'=2,'yl'=2,'c'=2,'x'=4,'yh'=4] {'x','yh','yl'}, dimensions={0} | all-to-all | bytes 425984 | tf_op jit(solution)/shard_map/all_to_all | solution.py:345
  63.6 0.1 relay.1
  63.7 17.9 %all_to_all.17.got = bf16[16,64,128]{2,1,0:T(8,128)(2,1)S(1)} all-to-all(bf16[16,64,128]{2,1,0:T(8,128)(2,1)S(1)} %relay.1), channel_id=1, replica_groups=mesh['zh'=4,'zl'=2,'yl'=2,'c'=2,'x'=4,'yh'=4] {'zh','zl','c'}, dimensions={0} | all-to-all | bytes 524288 | tf_op jit(solution)/shard_map/all_to_all | solution.py:355
  81.6 0.0 copy-done.3
  81.6 0.0 copy-done.9
  81.6 0.0 copy-done.12
  81.6 1.0 %finish.1 = (f32[2,512]{1,0:T(2,128)}, f32[32,32]{1,0:T(8,128)}) custom-call(bf16[16,64,128]{2,1,0:T(8,128)(2,1)S(1)} %all_to_all.17.got, bf16[64,512]{1,0:T(8,128)(2,1)S(1)} %get-tuple-element.9.pairs, bf16[2,16,1024]{2,1,0:T(8,128)(2,1)S(1)} %copy-done.3, bf16[2,512]{1,0:T(2,128)(2,1)S(1)} %copy-done.9, f32[2,16]{1,0:T(2,128)S(1)} %copy-done.12), custom_call_target="tpu_custom_call" | custom-call | tf_op jit(solution)/shard_map/finish/pallas_call | solution.py:356
Async XLA Ops:
  0.6 1.3 %copy-start = (f32[289,1024]{1,0:T(8,128)S(1)}, f32[289,1024]{1,0:T(8,128)}, u32[]{:S(2)}) copy-start(f32[289,1024]{1,0:T(8,128)} %high.1) | copy-start | bytes 3551236
  1.9 1.3 %copy-start.1 = (f32[289,1024]{1,0:T(8,128)S(1)}, f32[289,1024]{1,0:T(8,128)}, u32[]{:S(2)}) copy-start(f32[289,1024]{1,0:T(8,128)} %constant.39.clone.cos) | copy-start | bytes 3551236
  3.2 0.8 %copy-start.2 = (bf16[2,16,1024]{2,1,0:T(8,128)(2,1)S(1)}, bf16[2,16,1024]{2,1,0:T(8,128)(2,1)}, u32[]{:S(2)}) copy-start(bf16[2,16,1024]{2,1,0:T(8,128)(2,1)} %pe.3) | copy-start | bytes 196612
  4.1 0.7 copy-start.6
  4.8 0.7 copy-start.7
  5.5 0.7 copy-start.8
  6.2 0.7 copy-start.11
  6.8 0.7 copy-start.13
  7.5 40.0 %copy-start.4 = (bf16[64,1024]{1,0:T(8,128)(2,1)S(1)}, bf16[64,1024]{1,0:T(8,128)(2,1)}, u32[]{:S(2)}) copy-start(bf16[64,1024]{1,0:T(8,128)(2,1)} %constant.41.clone.second) | copy-start | bytes 393220
  7.5 40.0 %copy-start.5 = (bf16[64,1024]{1,0:T(8,128)(2,1)S(1)}, bf16[64,1024]{1,0:T(8,128)(2,1)}, u32[]{:S(2)}) copy-start(bf16[64,1024]{1,0:T(8,128)(2,1)} %constant.40.clone.first) | copy-start | bytes 393220
  7.5 40.0 %copy-start.10 = (f32[1024]{0:T(1024)S(1)}, f32[1024]{0:T(1024)}, u32[]{:S(2)}) copy-start(f32[1024]{0:T(1024)} %param.14) | copy-start | bytes 12292
  47.5 34.1 %copy-start.3 = (bf16[2,16,1024]{2,1,0:T(8,128)(2,1)S(1)}, bf16[2,16,1024]{2,1,0:T(8,128)(2,1)}, u32[]{:S(2)}) copy-start(bf16[2,16,1024]{2,1,0:T(8,128)(2,1)} %pe.3) | copy-start | bytes 196612
  47.5 34.1 %copy-start.9 = (bf16[2,512]{1,0:T(2,128)(2,1)S(1)}, bf16[2,512]{1,0:T(2,128)(2,1)}, u32[]{:S(2)}) copy-start(bf16[2,512]{1,0:T(2,128)(2,1)} %vec.3) | copy-start | bytes 6148
  47.5 34.1 %copy-start.12 = (f32[2,16]{1,0:T(2,128)S(1)}, f32[2,16]{1,0:T(2,128)}, u32[]{:S(2)}) copy-start(f32[2,16]{1,0:T(2,128)} %energy.3) | copy-start | bytes 388

commit v3 on v2

--- a/solution.py
+++ b/solution.py
@@ -104,8 +104,13 @@
 
 
 def pack_kernel(
-    mine, coords, cond, val, pe, vec, energy, low, high, cos, msg, pairs, gram, lam, wide, rows, lines
+    mine, coords, cond, val, pe, vec, energy, *refs
 ):
+    del mine
+    far, (msg, pairs, gram), near, (wide, rows, lines, sem) = refs[:3], refs[3:6], refs[6:9], refs[9:]
+    copies = [pltpu.make_async_copy(far[i], near[i], sem.at[i]) for i in range(3)]
+    for copy in copies:
+        copy.start()
     x = spread_vectors(vec, wide)
     for k in range(2):
         cf = cond[k].astype(f32)
@@ -125,7 +130,7 @@
     place = jnp.zeros((1, LANES), f32)
     for k in range(2):
         for s in range(2):
-            place = jnp.where(lane == 64 + 2 * k + s, coords[k, s].astype(f32), place)
+            place = jnp.where(lane == 64 + 2 * k + s, coords[k : k + 1, s : s + 1].astype(f32), place)
     lines[pl.ds(0, ND, stride=2), :] = dot_t(left, xp)
     lines[pl.ds(1, ND, stride=2), :] = dot_t(exchange_rows(pe), xd) + place
     msg[...] = lines[...].astype(bf16)
@@ -136,15 +141,31 @@
         precision=HIGH,
         preferred_element_type=f32,
     )
-    own = iota((NQ, LANES), 1) == mine[0] % LANES
+    for copy in copies:
+        copy.wait()
+
+
+def spectrum(mine, tiles, cos):
+    own = iota((NQ, LANES), 1) == mine % LANES
     out = []
-    for ref in (low, high):
-        column = jnp.sum(jnp.where(own, ref[...], 0.0), axis=1, keepdims=True)
-        out.append(jnp.sum(column * cos[...], axis=0, keepdims=True))
-    lam[...] = jnp.concatenate(out + [jnp.zeros((6, NK), f32)], axis=0)
-
-
-def spectral_kernel(where, got, lam, gram, coulomb, first, second, msg, lines, wide):
+    for g in range(2):
+        column = jnp.sum(jnp.where(own, tiles[g], 0.0), axis=1, keepdims=True)
+        line = jnp.sum(column * cos[...], axis=0, keepdims=True)
+        out.append(jnp.broadcast_to(line, (32, NK)))
+    return jnp.concatenate(out, axis=0)
+
+
+def spectral_kernel(
+    where, got, gram, coulomb, first, second, table, far, msg, lines, wide, tiles, cos, sem
+):
+    tile = pl.multiple_of((where[0] // LANES) * LANES, LANES)
+    copies = [
+        pltpu.make_async_copy(table.at[:, pl.ds(tile + g * HALF, LANES)], tiles.at[g], sem.at[g])
+        for g in range(2)
+    ]
+    copies.append(pltpu.make_async_copy(far, cos, sem.at[2]))
+    for copy in copies:
+        copy.start()
     lines[...] = got[...].astype(f32)
     proj = lines[pl.ds(0, ND, stride=2), :].astype(bf16)
     rest = lines[pl.ds(1, ND, stride=2), :]
@@ -162,9 +183,9 @@
         basis.append((hi, lo))
         part = (dot_t(proj, hi) + dot_t(proj, lo))[k * 64 : (k + 1) * 64]
         hat = part if hat is None else hat + part
-    scale = jnp.concatenate(
-        [jnp.broadcast_to(lam[0:1, :], (32, NK)), jnp.broadcast_to(lam[1:2, :], (32, NK))], axis=0
-    )
+    for copy in copies:
+        copy.wait()
+    scale = spectrum(where[0], tiles, cos)
     exact = hat * scale
     scaled = exact.astype(bf16)
     finer = (exact - scaled.astype(f32)).astype(bf16)
@@ -268,79 +289,89 @@
     return pltpu.CompilerParams(vmem_limit_bytes=mib << 20)
 
 
+def in_hbm(x):
+    return pltpu.with_memory_space_constraint(jnp.asarray(x), pltpu.HBM)
+
+
 def sds(shape, dtype):
     return jax.ShapeDtypeStruct(shape, dtype)
 
 
 def on_device(pair_exchange, conduction, valence, coulomb, screening, energies, vectors, k_coords):
     mine = (lax.axis_index(B) * NA + lax.axis_index(A)).reshape(1).astype(jnp.int32)
+    first, second = cas_tables()
+    near = [
+        in_hbm(v) for v in (k_coords, conduction, valence, pair_exchange, vectors, energies)
+    ] + [in_hbm(v) for v in (first, second, coulomb.reshape(8, LANES))]
+    any_space = pl.BlockSpec(memory_space=pl.ANY)
     fixed2 = lambda i, *w: (0, 0)
     fixed3 = lambda i, *w: (0, 0, 0)
-    msg, pairs, gram, lam = pl.pallas_call(
+    msg, pairs, gram, first, second, bare = pl.pallas_call(
         pack_kernel,
         out_shape=(
             sds((2 * ND, LANES), bf16),
             sds((64, HALF), bf16),
             sds((32, LANES), f32),
-            sds((8, NK), f32),
+            sds((64, NK), bf16),
+            sds((64, NK), bf16),
+            sds((8, LANES), f32),
         ),
         grid_spec=pltpu.PrefetchScalarGridSpec(
-            num_scalar_prefetch=2,
+            num_scalar_prefetch=1,
             grid=(1,),
             in_specs=[
+                pl.BlockSpec(k_coords.shape, fixed2),
                 pl.BlockSpec(conduction.shape, fixed3),
                 pl.BlockSpec(valence.shape, fixed3),
                 pl.BlockSpec(pair_exchange.shape, fixed3),
                 pl.BlockSpec(vectors.shape, fixed2),
                 pl.BlockSpec(energies.shape, fixed2),
-                pl.BlockSpec((NQ, LANES), lambda i, w, c: (0, w[0] // LANES)),
-                pl.BlockSpec((NQ, LANES), lambda i, w, c: (0, w[0] // LANES + HALF // LANES)),
-                pl.BlockSpec((NQ, NK), fixed2),
+                any_space,
+                any_space,
+                any_space,
             ],
             out_specs=[
                 pl.BlockSpec((2 * ND, LANES), fixed2),
                 pl.BlockSpec((64, HALF), fixed2),
                 pl.BlockSpec((32, LANES), fixed2),
-                pl.BlockSpec((8, NK), fixed2),
+                pl.BlockSpec((64, NK), fixed2),
+                pl.BlockSpec((64, NK), fixed2),
+                pl.BlockSpec((8, LANES), fixed2),
             ],
             scratch_shapes=[
                 pltpu.VMEM((32, LANES), f32),
                 pltpu.VMEM((64, HALF), f32),
                 pltpu.VMEM((2 * ND, LANES), f32),
+                pltpu.SemaphoreType.DMA((3,)),
             ],
         ),
         compiler_params=room(12),
         name="pack",
-    )(
-        mine,
-        k_coords,
-        conduction,
-        valence,
-        pair_exchange,
-        vectors,
-        energies,
-        screening,
-        screening,
-        cos_table(),
-    )
+    )(mine, *near)
     got = lax.all_to_all(msg.reshape(ND, 2, LANES), B + A, 0, 0, tiled=True)
-    first, second = cas_tables()
     out = pl.pallas_call(
         spectral_kernel,
         out_shape=sds((NA * ROWS, LANES), bf16),
-        in_specs=[smem()] + [vmem()] * 6,
+        in_specs=[smem()] + [vmem()] * 5 + [any_space] * 2,
         out_specs=vmem(),
-        scratch_shapes=[pltpu.VMEM((2 * ND, LANES), f32), pltpu.VMEM((32, LANES), f32)],
+        scratch_shapes=[
+            pltpu.VMEM((2 * ND, LANES), f32),
+            pltpu.VMEM((32, LANES), f32),
+            pltpu.VMEM((2, NQ, LANES), f32),
+            pltpu.VMEM((NQ, NK), f32),
+            pltpu.SemaphoreType.DMA((3,)),
+        ],
         compiler_params=room(28),
         name="spectral",
     )(
         mine,
         got.reshape(2 * ND, LANES),
-        lam,
         gram,
-        coulomb.reshape(8, LANES),
+        bare,
         first,
         second,
+        in_hbm(screening),
+        in_hbm(cos_table()),
     )
     got = lax.all_to_all(out.reshape(NA, ROWS // 2, 2, LANES), A, 0, 0, tiled=True)
     out = pl.pallas_call(

time: 83.1 us -> 77.4 us (0.931)
  local copies, waits for them, and re-layouts: 6.89 us -> 0.02 us
  Pallas kernels: 5.56 us -> 6.78 us
    unnamed x28 -> x6, local copies, waits for them, and re-layouts: 6.89 us -> 0.02 us
where the time goes in v3:
time: 77.4 us; the launch traced here: 77.1 us
  blocking collectives  69.6 us (90%)
  Pallas kernels  6.78 us (9%)
    all_to_all x1, blocking collectives, on_device(): got = lax.all_to_all(msg.reshape(ND, 2, LANES), B + A, 0, 0, tiled=True)  38.8 us
    all_to_all x1, blocking collectives, on_device(): got = lax.all_to_all(out, B, 0, 0, tiled=True)  17.9 us
    all_to_all x1, blocking collectives, on_device(): lax.all_to_all(out.reshape(NA, ROWS // 2, 2, LANES), A, 0, 0, tiled=True)  12.9 us
    pallas_call x1, Pallas kernels, on_device(): pl.pallas_call(spectral_kernel, out_shape=sds((NA * ROWS, LANES), bf16),...  3.83 us
    pallas_call x1, Pallas kernels, on_device(): pl.pallas_call(pack_kernel, out_shape=(sds((2 * ND, LANES), bf16), sds((6...  1.86 us

profile of v3, /device:TPU:1, one launch (start us, length us, event | category | flops | bytes accessed | tf_op | source)
XLA Modules:
  0.0 77.1 jit_solution(470029384026757864)
XLA Ops:
  0.6 1.9 %pack.1 = (bf16[1024,128]{1,0:T(8,128)(2,1)S(1)}, bf16[64,512]{1,0:T(8,128)(2,1)S(1)}, f32[32,128]{1,0:T(8,128)S(1)}, bf16[64,1024]{1,0:T(8,128)(2,1)S(1)}, bf16...) custom-call(s32[1]{0:T(128)} %bitcast.mine.where, s32[2,2]{1,0:T(2,128)} %coords.1, bf16[2,4,1024]{2,1,0:T(4,128)(2,1)} %cond.1, ...), custom_call_target="tpu_custom_call" | custom-call | tf_op jit(solution)/shard_map/pack/pallas_call | solution.py:309
  2.5 38.8 %all_to_all.15 = bf16[512,2,128]{2,1,0:T(2,128)(2,1)S(1)} all-to-all(bf16[512,2,128]{2,1,0:T(2,128)(2,1)S(1)} %bitcast.9), channel_id=1, replica_groups=mesh['zh'=4,'zl'=2,'yl'=2,'c'=2,'x'=4,'yh'=4] {'zh','zl','c','x','yh','yl'}, dimensions={0} | all-to-all | bytes 524288 | tf_op jit(solution)/shard_map/all_to_all | solution.py:351
  41.3 3.8 %spectral.1 = bf16[832,128]{1,0:T(8,128)(2,1)S(1)} custom-call(s32[1]{0:T(128)} %bitcast.mine.where, bf16[1024,128]{1,0:T(8,128)(2,1)S(1)} %bitcast.6, f32[32,128]{1,0:T(8,128)S(1)} %get-tuple-element.9.gram, f32[8,128]{1,0:T(8,128)S(1)} %get-tuple-element.10.coulomb, bf16[64,1024]{1,0:T(8,128)(2,1)S(1)} %get-tuple-element.11.first, ...), custom_call_target="tpu_custom_call" | custom-call | tf_op jit(solution)/shard_map/spectral/pallas_call | solution.py:352
  45.2 0.0 copy-start
  45.2 0.0 copy-start.1
  45.2 0.0 copy-start.2
  45.2 12.9 %all_to_all.16 = bf16[32,13,2,128]{3,2,1,0:T(2,128)(2,1)S(1)} all-to-all(bf16[32,13,2,128]{3,2,1,0:T(2,128)(2,1)S(1)} %bitcast.8), channel_id=1, replica_groups=mesh['zh'=4,'zl'=2,'yl'=2,'c'=2,'x'=4,'yh'=4] {'x','yh','yl'}, dimensions={0} | all-to-all | bytes 425984 | tf_op jit(solution)/shard_map/all_to_all | solution.py:376
  58.1 0.1 relay.1
  58.2 17.9 %all_to_all.17.got = bf16[16,64,128]{2,1,0:T(8,128)(2,1)S(1)} all-to-all(bf16[16,64,128]{2,1,0:T(8,128)(2,1)S(1)} %relay.1), channel_id=1, replica_groups=mesh['zh'=4,'zl'=2,'yl'=2,'c'=2,'x'=4,'yh'=4] {'zh','zl','c'}, dimensions={0} | all-to-all | bytes 524288 | tf_op jit(solution)/shard_map/all_to_all | solution.py:386
  76.1 0.0 copy-done
  76.1 0.0 copy-done.1
  76.1 0.0 copy-done.2
  76.1 1.0 %finish.1 = (f32[2,512]{1,0:T(2,128)}, f32[32,32]{1,0:T(8,128)}) custom-call(bf16[16,64,128]{2,1,0:T(8,128)(2,1)S(1)} %all_to_all.17.got, bf16[64,512]{1,0:T(8,128)(2,1)S(1)} %get-tuple-element.13.pairs, bf16[2,16,1024]{2,1,0:T(8,128)(2,1)S(1)} %copy-done, bf16[2,512]{1,0:T(2,128)(2,1)S(1)} %copy-done.1, f32[2,16]{1,0:T(2,128)S(1)} %copy-done.2), custom_call_target="tpu_custom_call" | custom-call | tf_op jit(solution)/shard_map/finish/pallas_call | solution.py:387
Async XLA Ops:
  45.2 30.9 %copy-start = (bf16[2,16,1024]{2,1,0:T(8,128)(2,1)S(1)}, bf16[2,16,1024]{2,1,0:T(8,128)(2,1)}, u32[]{:S(2)}) copy-start(bf16[2,16,1024]{2,1,0:T(8,128)(2,1)} %pe.3) | copy-start | bytes 196612
  45.2 30.9 %copy-start.1 = (bf16[2,512]{1,0:T(2,128)(2,1)S(1)}, bf16[2,512]{1,0:T(2,128)(2,1)}, u32[]{:S(2)}) copy-start(bf16[2,512]{1,0:T(2,128)(2,1)} %vec.3) | copy-start | bytes 6148
  45.2 30.9 %copy-start.2 = (f32[2,16]{1,0:T(2,128)S(1)}, f32[2,16]{1,0:T(2,128)}, u32[]{:S(2)}) copy-start(f32[2,16]{1,0:T(2,128)} %energy.3) | copy-start | bytes 388

commit v4 on v3

--- a/solution.py
+++ b/solution.py
@@ -17,13 +17,15 @@
 NQ = 289
 NAMES = ("zh", "zl", "yl", "c", "x", "yh")
 SIZES = (4, 2, 2, 2, 4, 4)
-A = ("x", "yh", "yl")
-B = ("zh", "zl", "c")
-NA = 32
-NBB = 16
+A = ("zh", "zl", "yh", "yl")
+B = ("x", "c")
+NA = 64
+NBB = 8
 ND = NA * NBB
 HALF = NG // 2
-ROWS = 26
+ROWS = NBB + 10
+FIELD = NA + NA // 2
+WIDE = FIELD + 16
 LANES = 128
 
 f32 = jnp.float32
@@ -166,7 +168,7 @@
     copies.append(pltpu.make_async_copy(far, cos, sem.at[2]))
     for copy in copies:
         copy.start()
-    lines[...] = got[...].astype(f32)
+    lines[0 : 2 * ND, :] = got[...].astype(f32)
     proj = lines[pl.ds(0, ND, stride=2), :].astype(bf16)
     rest = lines[pl.ds(1, ND, stride=2), :]
     basis = []
@@ -236,19 +238,19 @@
     alpha = jnp.concatenate(alpha, axis=0)
     hi = alpha.astype(bf16).astype(f32)
     cd = lines[pl.ds(NBB + 8, NA, stride=ROWS), :]
-    cd = cd[0:16] + pltpu.roll(cd[16:32], 64, 1)
+    cd = cd[0 : NA // 2] + pltpu.roll(cd[NA // 2 :], 64, 1)
     tail = jnp.concatenate([cd, hi, alpha - hi], axis=0).astype(bf16)
     for b in range(NBB):
-        msg[b, 0:32, :] = lines[pl.ds(b, NA, stride=ROWS), :].astype(bf16)
-        msg[b, 32:64, :] = tail
+        msg[b, 0:NA, :] = lines[pl.ds(b, NA, stride=ROWS), :].astype(bf16)
+        msg[b, NA:WIDE, :] = tail
 
 
 def finish_kernel(got, pairs, pe, vec, energy, out, alpha_out, wide, rows):
     x = spread_vectors(vec, wide)
-    potential = got[:, 0:32, :].reshape(ND, LANES)
+    potential = got[:, 0:NA, :].reshape(ND, LANES)
     field = []
     for b in range(NBB):
-        part = got[b, 32:48, :].astype(f32)
+        part = got[b, NA:FIELD, :].astype(f32)
         field += [part, pltpu.roll(part, 64, 1)]
     field = jnp.concatenate(field, axis=0).astype(bf16)
     direct = jnp.dot(pairs[...], potential, preferred_element_type=f32)
@@ -260,7 +262,7 @@
     applied = energy_column(energy) * x + (2.0 / NT) * exchange - direct / NK
     alpha = jnp.zeros((16, LANES), f32)
     for b in range(NBB):
-        alpha = alpha + got[b, 48:64, :].astype(f32)
+        alpha = alpha + got[b, FIELD:WIDE, :].astype(f32)
     alpha = alpha[0:8] + alpha[8:16]
     for c in range(4):
         wide[pl.ds(c, 8, stride=4), :] = alpha
@@ -355,7 +357,7 @@
         in_specs=[smem()] + [vmem()] * 5 + [any_space] * 2,
         out_specs=vmem(),
         scratch_shapes=[
-            pltpu.VMEM((2 * ND, LANES), f32),
+            pltpu.VMEM((max(2 * ND, NA * ROWS), LANES), f32),
             pltpu.VMEM((32, LANES), f32),
             pltpu.VMEM((2, NQ, LANES), f32),
             pltpu.VMEM((NQ, NK), f32),
@@ -376,7 +378,7 @@
     got = lax.all_to_all(out.reshape(NA, ROWS // 2, 2, LANES), A, 0, 0, tiled=True)
     out = pl.pallas_call(
         relay_kernel,
-        out_shape=sds((NBB, 64, LANES), bf16),
+        out_shape=sds((NBB, WIDE, LANES), bf16),
         in_specs=[vmem()],
         out_specs=vmem(),
         scratch_shapes=[pltpu.VMEM((NA * ROWS, LANES), f32)],

time: 77.4 us -> 76.5 us (0.988)
  blocking collectives: 69.6 us -> 68.7 us
    all_to_all x1, blocking collectives: 17.9 us -> 11.9 us  [on_device(): got = lax.all_to_all(out, B, 0, 0, tiled=True)]
    all_to_all x1, blocking collectives: 12.9 us -> 17.5 us  [on_device(): lax.all_to_all(out.reshape(NA, ROWS // 2, 2, LANES), A, 0, 0, tiled=True)]
where the time goes in v4:
time: 76.5 us; the launch traced here: 76.2 us
  blocking collectives  68.7 us (90%)
  Pallas kernels  6.8 us (9%)
    all_to_all x1, blocking collectives, on_device(): got = lax.all_to_all(msg.reshape(ND, 2, LANES), B + A, 0, 0, tiled=True)  39.3 us
    all_to_all x1, blocking collectives, on_device(): lax.all_to_all(out.reshape(NA, ROWS // 2, 2, LANES), A, 0, 0, tiled=True)  17.5 us
    all_to_all x1, blocking collectives, on_device(): got = lax.all_to_all(out, B, 0, 0, tiled=True)  11.9 us
    pallas_call x1, Pallas kernels, on_device(): pl.pallas_call(spectral_kernel, out_shape=sds((NA * ROWS, LANES), bf16),...  3.84 us
    pallas_call x1, Pallas kernels, on_device(): pl.pallas_call(pack_kernel, out_shape=(sds((2 * ND, LANES), bf16), sds((6...  1.86 us

profile of v4, /device:TPU:1, one launch (start us, length us, event | category | flops | bytes accessed | tf_op | source)
XLA Modules:
  0.0 76.2 jit_solution(3327648142393577086)
XLA Ops:
  0.6 1.9 %pack.1 = (bf16[1024,128]{1,0:T(8,128)(2,1)S(1)}, bf16[64,512]{1,0:T(8,128)(2,1)S(1)}, f32[32,128]{1,0:T(8,128)S(1)}, bf16[64,1024]{1,0:T(8,128)(2,1)S(1)}, bf16...) custom-call(s32[1]{0:T(128)} %bitcast.mine.where, s32[2,2]{1,0:T(2,128)} %coords.1, bf16[2,4,1024]{2,1,0:T(4,128)(2,1)} %cond.1, ...), custom_call_target="tpu_custom_call" | custom-call | tf_op jit(solution)/shard_map/pack/pallas_call | solution.py:311
  2.5 39.3 %all_to_all.15 = bf16[512,2,128]{2,1,0:T(2,128)(2,1)S(1)} all-to-all(bf16[512,2,128]{2,1,0:T(2,128)(2,1)S(1)} %bitcast.9), channel_id=1, replica_groups=mesh['zh'=4,'zl'=2,'yl'=2,'c'=2,'x'=4,'yh'=4] {'x','c','zh','zl','yh','yl'}, dimensions={0} | all-to-all | bytes 524288 | tf_op jit(solution)/shard_map/all_to_all | solution.py:353
  41.8 3.8 %spectral.1 = bf16[1152,128]{1,0:T(8,128)(2,1)S(1)} custom-call(s32[1]{0:T(128)} %bitcast.mine.where, bf16[1024,128]{1,0:T(8,128)(2,1)S(1)} %bitcast.8, f32[32,128]{1,0:T(8,128)S(1)} %get-tuple-element.9.gram, f32[8,128]{1,0:T(8,128)S(1)} %get-tuple-element.10.coulomb, bf16[64,1024]{1,0:T(8,128)(2,1)S(1)} %get-tuple-element.11.first, ...), custom_call_target="tpu_custom_call" | custom-call | tf_op jit(solution)/shard_map/spectral/pallas_call | solution.py:354
  45.6 0.0 copy-start
  45.6 0.0 copy-start.1
  45.7 0.0 copy-start.2
  45.7 17.5 %all_to_all.16 = bf16[64,9,2,128]{3,2,1,0:T(2,128)(2,1)S(1)} all-to-all(bf16[64,9,2,128]{3,2,1,0:T(2,128)(2,1)S(1)} %bitcast.7), channel_id=1, replica_groups=mesh['zh'=4,'zl'=2,'yl'=2,'c'=2,'x'=4,'yh'=4] {'zh','zl','yh','yl'}, dimensions={0} | all-to-all | bytes 589824 | tf_op jit(solution)/shard_map/all_to_all | solution.py:378
  63.2 0.1 relay.1
  63.3 11.9 %all_to_all.17.got = bf16[8,112,128]{2,1,0:T(8,128)(2,1)S(1)} all-to-all(bf16[8,112,128]{2,1,0:T(8,128)(2,1)S(1)} %relay.1), channel_id=1, replica_groups=mesh['zh'=4,'zl'=2,'yl'=2,'c'=2,'x'=4,'yh'=4] {'x','c'}, dimensions={0} | all-to-all | bytes 458752 | tf_op jit(solution)/shard_map/all_to_all | solution.py:388
  75.2 0.0 copy-done
  75.2 0.0 copy-done.1
  75.2 0.0 copy-done.2
  75.2 1.0 %finish.1 = (f32[2,512]{1,0:T(2,128)}, f32[32,32]{1,0:T(8,128)}) custom-call(bf16[8,112,128]{2,1,0:T(8,128)(2,1)S(1)} %all_to_all.17.got, bf16[64,512]{1,0:T(8,128)(2,1)S(1)} %get-tuple-element.13.pairs, bf16[2,16,1024]{2,1,0:T(8,128)(2,1)S(1)} %copy-done, bf16[2,512]{1,0:T(2,128)(2,1)S(1)} %copy-done.1, f32[2,16]{1,0:T(2,128)S(1)} %copy-done.2), custom_call_target="tpu_custom_call" | custom-call | tf_op jit(solution)/shard_map/finish/pallas_call | solution.py:389
Async XLA Ops:
  45.6 29.5 %copy-start = (bf16[2,16,1024]{2,1,0:T(8,128)(2,1)S(1)}, bf16[2,16,1024]{2,1,0:T(8,128)(2,1)}, u32[]{:S(2)}) copy-start(bf16[2,16,1024]{2,1,0:T(8,128)(2,1)} %pe.3) | copy-start | bytes 196612
  45.6 29.5 %copy-start.1 = (bf16[2,512]{1,0:T(2,128)(2,1)S(1)}, bf16[2,512]{1,0:T(2,128)(2,1)}, u32[]{:S(2)}) copy-start(bf16[2,512]{1,0:T(2,128)(2,1)} %vec.3) | copy-start | bytes 6148
  45.7 29.5 %copy-start.2 = (f32[2,16]{1,0:T(2,128)S(1)}, f32[2,16]{1,0:T(2,128)}, u32[]{:S(2)}) copy-start(f32[2,16]{1,0:T(2,128)} %energy.3) | copy-start | bytes 388

commit v5 on v4

--- a/solution.py
+++ b/solution.py
@@ -15,12 +15,13 @@
 NV = 32
 NT = NK * NB
 NQ = 289
+CHUNK = 256
 NAMES = ("zh", "zl", "yl", "c", "x", "yh")
 SIZES = (4, 2, 2, 2, 4, 4)
-A = ("zh", "zl", "yh", "yl")
-B = ("x", "c")
-NA = 64
-NBB = 8
+A = ("zh", "zl", "yh")
+B = ("x", "yl", "c")
+NA = 32
+NBB = 16
 ND = NA * NBB
 HALF = NG // 2
 ROWS = NBB + 10
@@ -39,21 +40,19 @@
     return np.concatenate([hi, lo], axis=0)
 
 
-def cas_tables():
+def tables():
     m = np.arange(32)
     phase = 2.0 * np.pi * ((m[:, None] * m[None, :]) % 32) / 32.0
     cas = np.cos(phase) + np.sin(phase)
-    first = np.repeat(cas, 32, axis=1)
-    second = np.tile(cas, (1, 32)) / 32.0
-    return split_table(first), split_table(second)
-
-
-def cos_table():
+    first = split_table(np.repeat(cas, 32, axis=1))
+    second = split_table(np.tile(cas, (1, 4)) / 32.0)
     f = np.arange(17)
-    m = np.arange(32)
     weight = np.where((f == 0) | (f == 16), 1.0, 2.0)
-    c = weight[:, None] * np.cos(2.0 * np.pi * ((f[:, None] * m[None, :]) % 32) / 32.0)
-    return np.einsum("im,jn->ijmn", c, c).reshape(NQ, NK).astype(np.float32)
+    cos = weight[:, None] * np.cos(2.0 * np.pi * ((f[:, None] * m[None, :]) % 32) / 32.0)
+    outer = np.zeros((24, NK), np.float32)
+    outer[0:17] = np.repeat(cos, 32, axis=1)
+    inner = np.tile(cos, (17, 4)).astype(np.float32)
+    return first, second, outer, inner
 
 
 def iota(shape, axis):
@@ -105,14 +104,36 @@
     return lax.dot_general(x, y, (((1,), (1,)), ((), ())), preferred_element_type=f32)
 
 
-def pack_kernel(
-    mine, coords, cond, val, pe, vec, energy, *refs
-):
-    del mine
-    far, (msg, pairs, gram), near, (wide, rows, lines, sem) = refs[:3], refs[3:6], refs[6:9], refs[9:]
-    copies = [pltpu.make_async_copy(far[i], near[i], sem.at[i]) for i in range(3)]
+def spectrum(lane_at, tiles, outer, inner):
+    own = iota((NQ, LANES), 1) == lane_at
+    pick = jnp.where(iota((24, NQ), 0) == iota((24, NQ), 1) // 17, 1.0, 0.0)
+    out = []
+    for g in range(2):
+        column = jnp.sum(jnp.where(own, tiles[g], 0.0), axis=1, keepdims=True)
+        part = jnp.dot(pick, column * inner[...], precision=HIGH, preferred_element_type=f32)
+        line = [
+            jnp.sum(outer[:, j * LANES : (j + 1) * LANES] * part, axis=0, keepdims=True)
+            for j in range(NK // LANES)
+        ]
+        out.append(jnp.concatenate(line, axis=1))
+    return out
+
+
+def pack_kernel(*refs):
+    far, (msg, pairs, gram, lam, first, second) = refs[:12], refs[12:18]
+    coords, cond, val, vec, pe, energy, tiles, bare, outer, inner, wide, rows, lines, sem = refs[18:]
+    mine = lax.axis_index(B) * NA + lax.axis_index(A)
+    tile = pl.multiple_of((mine // LANES) * LANES, LANES)
+    near = (coords, cond, val, vec, pe, energy, inner, outer, bare, first, second)
+    pairs_of = list(zip(far[:6] + far[7:], near))
+    pairs_of += [(far[6].at[:, pl.ds(tile + g * HALF, LANES)], tiles.at[g]) for g in range(2)]
+    copies = [
+        pltpu.make_async_copy(src, dst, sem.at[i]) for i, (src, dst) in enumerate(pairs_of)
+    ]
     for copy in copies:
         copy.start()
+    for copy in copies[:6]:
+        copy.wait()
     x = spread_vectors(vec, wide)
     for k in range(2):
         cf = cond[k].astype(f32)
@@ -143,74 +164,70 @@
         precision=HIGH,
         preferred_element_type=f32,
     )
-    for copy in copies:
+    for copy in copies[6:]:
         copy.wait()
-
-
-def spectrum(mine, tiles, cos):
-    own = iota((NQ, LANES), 1) == mine % LANES
-    out = []
+    index = iota((8, LANES), 0) * LANES + iota((8, LANES), 1)
+    lines_of = spectrum(mine - tile, tiles, outer, inner)
     for g in range(2):
-        column = jnp.sum(jnp.where(own, tiles[g], 0.0), axis=1, keepdims=True)
-        line = jnp.sum(column * cos[...], axis=0, keepdims=True)
-        out.append(jnp.broadcast_to(line, (32, NK)))
-    return jnp.concatenate(out, axis=0)
-
-
-def spectral_kernel(
-    where, got, gram, coulomb, first, second, table, far, msg, lines, wide, tiles, cos, sem
-):
-    tile = pl.multiple_of((where[0] // LANES) * LANES, LANES)
-    copies = [
-        pltpu.make_async_copy(table.at[:, pl.ds(tile + g * HALF, LANES)], tiles.at[g], sem.at[g])
-        for g in range(2)
-    ]
-    copies.append(pltpu.make_async_copy(far, cos, sem.at[2]))
-    for copy in copies:
-        copy.start()
+        factor = jnp.sum(jnp.where(index == mine + g * HALF, bare[...], 0.0), keepdims=True)
+        lines_of.append(jnp.broadcast_to(factor, (1, NK)))
+    lam[...] = jnp.concatenate(lines_of + [jnp.zeros((4, NK), f32)], axis=0)
+
+
+def spectral_kernel(got, gram, lam, first, second, msg, lines, wide):
     lines[0 : 2 * ND, :] = got[...].astype(f32)
-    proj = lines[pl.ds(0, ND, stride=2), :].astype(bf16)
+    proj = jnp.transpose(lines[pl.ds(0, ND, stride=2), :]).astype(bf16)
     rest = lines[pl.ds(1, ND, stride=2), :]
-    basis = []
-    hat = None
     slot = iota((ND, 64), 1) % 32
+    at_first, from_second = [], []
     for k in range(2):
         at = [rest[:, 64 + 2 * k + s : 65 + 2 * k + s].astype(jnp.int32) for s in range(2)]
         ones = [jnp.where(slot == p, 1.0, 0.0).astype(bf16) for p in at]
-        ta = jnp.dot(ones[0], first[...], preferred_element_type=f32)
+        at_first.append(ones[0])
         tb = jnp.dot(ones[1], second[...], preferred_element_type=f32)
-        exact = ta * tb
-        hi = exact.astype(bf16)
-        lo = (exact - hi.astype(f32)).astype(bf16)
-        basis.append((hi, lo))
-        part = (dot_t(proj, hi) + dot_t(proj, lo))[k * 64 : (k + 1) * 64]
-        hat = part if hat is None else hat + part
-    for copy in copies:
-        copy.wait()
-    scale = spectrum(where[0], tiles, cos)
-    exact = hat * scale
-    scaled = exact.astype(bf16)
-    finer = (exact - scaled.astype(f32)).astype(bf16)
-    hat = hat.astype(bf16)
-    both = jnp.concatenate([scaled, finer], axis=0)
-    side = iota((ND, LANES), 1) // 64
-    back = []
-    for hi, lo in basis:
-        r = dot_nt(hi, both)
-        back.append(r + pltpu.roll(r, 64, 1) + dot_nt(lo, jnp.concatenate([scaled] * 2, axis=0)))
-    back = jnp.where(side == 0, back[0], back[1])
+        from_second.append(jnp.concatenate([tb] * (CHUNK // LANES), axis=1))
+    back = [None, None]
+    direct = None
+    for m in range(0, NK, CHUNK):
+        hat = None
+        basis = []
+        for k in range(2):
+            ta = jnp.dot(at_first[k], first[:, m : m + CHUNK], preferred_element_type=f32)
+            exact = ta * from_second[k]
+            hi = exact.astype(bf16)
+            lo = (exact - hi.astype(f32)).astype(bf16)
+            basis.append((hi, lo))
+            mine = proj[k * 64 : (k + 1) * 64]
+            part = jnp.dot(mine, hi, preferred_element_type=f32) + jnp.dot(
+                mine, lo, preferred_element_type=f32
+            )
+            hat = part if hat is None else hat + part
+        scale = jnp.concatenate(
+            [jnp.broadcast_to(lam[g : g + 1, m : m + CHUNK], (32, CHUNK)) for g in range(2)], axis=0
+        )
+        exact = hat * scale
+        scaled = exact.astype(bf16)
+        finer = (exact - scaled.astype(f32)).astype(bf16)
+        hat = hat.astype(bf16)
+        both = jnp.concatenate([scaled, finer], axis=0)
+        again = jnp.concatenate([scaled, jnp.zeros((64, CHUNK), bf16)], axis=0)
+        for k in range(2):
+            part = dot_nt(basis[k][0], both) + dot_nt(basis[k][1], again)
+            back[k] = part if back[k] is None else back[k] + part
+        part = dot_nt(hat[0:32], jnp.concatenate([scaled[0:32]] * 4, axis=0)) + dot_nt(
+            hat[32:64], jnp.concatenate([scaled[32:64]] * 4, axis=0)
+        )
+        direct = part if direct is None else direct + part
+    back = [r + pltpu.roll(r, 64, 1) for r in back]
+    back = jnp.where(iota((ND, LANES), 1) < 64, back[0], back[1])
     for b in range(NBB):
         lines[pl.ds(b, NA, stride=ROWS), :] = back[b * NA : (b + 1) * NA]
-    direct = dot_nt(hat[0:32], jnp.concatenate([scaled[0:32]] * 4, axis=0)) + dot_nt(
-        hat[32:64], jnp.concatenate([scaled[32:64]] * 4, axis=0)
-    )
     lane = iota((1, LANES), 1)
     dens = jnp.sum(rest, axis=0, keepdims=True)
-    index = iota((8, LANES), 0) * LANES + iota((8, LANES), 1)
     outer = jnp.zeros((32, LANES), f32)
     cd = jnp.zeros((1, LANES), f32)
     for g in range(2):
-        factor = jnp.sum(jnp.where(index == where[0] + g * HALF, coulomb[...], 0.0), keepdims=True)
+        factor = lam[2 + g : 3 + g, 0:LANES]
         own = jnp.where(lane // 32 == g, dens, 0.0)
         row = block_sum(own)
         column = jnp.sum(
@@ -283,10 +300,6 @@
     return pl.BlockSpec(memory_space=pltpu.VMEM)
 
 
-def smem():
-    return pl.BlockSpec(memory_space=pltpu.SMEM)
-
-
 def room(mib):
     return pltpu.CompilerParams(vmem_limit_bytes=mib << 20)
 
@@ -300,81 +313,50 @@
 
 
 def on_device(pair_exchange, conduction, valence, coulomb, screening, energies, vectors, k_coords):
-    mine = (lax.axis_index(B) * NA + lax.axis_index(A)).reshape(1).astype(jnp.int32)
-    first, second = cas_tables()
-    near = [
-        in_hbm(v) for v in (k_coords, conduction, valence, pair_exchange, vectors, energies)
-    ] + [in_hbm(v) for v in (first, second, coulomb.reshape(8, LANES))]
+    first, second, outer, inner = tables()
+    far = (k_coords, conduction, valence, vectors, pair_exchange, energies, screening)
+    far += (inner, outer, coulomb.reshape(8, LANES), first, second)
     any_space = pl.BlockSpec(memory_space=pl.ANY)
-    fixed2 = lambda i, *w: (0, 0)
-    fixed3 = lambda i, *w: (0, 0, 0)
-    msg, pairs, gram, first, second, bare = pl.pallas_call(
+    own = [pltpu.VMEM(v.shape, v.dtype) for v in far[:6]]
+    msg, pairs, gram, lam, first, second = pl.pallas_call(
         pack_kernel,
         out_shape=(
             sds((2 * ND, LANES), bf16),
             sds((64, HALF), bf16),
             sds((32, LANES), f32),
+            sds((8, NK), f32),
             sds((64, NK), bf16),
-            sds((64, NK), bf16),
-            sds((8, LANES), f32),
+            sds((64, LANES), bf16),
         ),
-        grid_spec=pltpu.PrefetchScalarGridSpec(
-            num_scalar_prefetch=1,
-            grid=(1,),
-            in_specs=[
-                pl.BlockSpec(k_coords.shape, fixed2),
-                pl.BlockSpec(conduction.shape, fixed3),
-                pl.BlockSpec(valence.shape, fixed3),
-                pl.BlockSpec(pair_exchange.shape, fixed3),
-                pl.BlockSpec(vectors.shape, fixed2),
-                pl.BlockSpec(energies.shape, fixed2),
-                any_space,
-                any_space,
-                any_space,
-            ],
-            out_specs=[
-                pl.BlockSpec((2 * ND, LANES), fixed2),
-                pl.BlockSpec((64, HALF), fixed2),
-                pl.BlockSpec((32, LANES), fixed2),
-                pl.BlockSpec((64, NK), fixed2),
-                pl.BlockSpec((64, NK), fixed2),
-                pl.BlockSpec((8, LANES), fixed2),
-            ],
-            scratch_shapes=[
-                pltpu.VMEM((32, LANES), f32),
-                pltpu.VMEM((64, HALF), f32),
-                pltpu.VMEM((2 * ND, LANES), f32),
-                pltpu.SemaphoreType.DMA((3,)),
-            ],
-        ),
+        in_specs=[any_space] * len(far),
+        out_specs=(vmem(),) * 6,
+        scratch_shapes=own
+        + [
+            pltpu.VMEM((2, NQ, LANES), f32),
+            pltpu.VMEM((8, LANES), f32),
+            pltpu.VMEM((24, NK), f32),
+            pltpu.VMEM((NQ, LANES), f32),
+            pltpu.VMEM((32, LANES), f32),
+            pltpu.VMEM((64, HALF), f32),
+            pltpu.VMEM((2 * ND, LANES), f32),
+            pltpu.SemaphoreType.DMA((13,)),
+        ],
         compiler_params=room(12),
         name="pack",
-    )(mine, *near)
+    )(*[in_hbm(v) for v in far])
     got = lax.all_to_all(msg.reshape(ND, 2, LANES), B + A, 0, 0, tiled=True)
     out = pl.pallas_call(
         spectral_kernel,
         out_shape=sds((NA * ROWS, LANES), bf16),
-        in_specs=[smem()] + [vmem()] * 5 + [any_space] * 2,
+        in_specs=[vmem()] * 5,
         out_specs=vmem(),
         scratch_shapes=[
             pltpu.VMEM((max(2 * ND, NA * ROWS), LANES), f32),
             pltpu.VMEM((32, LANES), f32),
-            pltpu.VMEM((2, NQ, LANES), f32),
-            pltpu.VMEM((NQ, NK), f32),
-            pltpu.SemaphoreType.DMA((3,)),
         ],
         compiler_params=room(28),
         name="spectral",
-    )(
-        mine,
-        got.reshape(2 * ND, LANES),
-        gram,
-        bare,
-        first,
-        second,
-        in_hbm(screening),
-        in_hbm(cos_table()),
-    )
+    )(got.reshape(2 * ND, LANES), gram, lam, first, second)
     got = lax.all_to_all(out.reshape(NA, ROWS // 2, 2, LANES), A, 0, 0, tiled=True)
     out = pl.pallas_call(
         relay_kernel,

time: 76.5 us -> 75.7 us (0.990)
  blocking collectives: 68.7 us -> 67.6 us
    all_to_all x1, blocking collectives: 17.5 us -> 15.9 us  [on_device(): lax.all_to_all(out.reshape(NA, ROWS // 2, 2, LANES), A, 0, 0, tiled=True)]
    all_to_all x1, blocking collectives: 11.9 us -> 12.9 us  [on_device(): got = lax.all_to_all(out, B, 0, 0, tiled=True)]
where the time goes in v5:
time: 75.7 us; the launch traced here: 75.5 us
  blocking collectives  67.6 us (89%)
  Pallas kernels  7.2 us (10%)
    all_to_all x1, blocking collectives, on_device(): got = lax.all_to_all(msg.reshape(ND, 2, LANES), B + A, 0, 0, tiled=True)  38.7 us
    all_to_all x1, blocking collectives, on_device(): lax.all_to_all(out.reshape(NA, ROWS // 2, 2, LANES), A, 0, 0, tiled=True)  15.9 us
    all_to_all x1, blocking collectives, on_device(): got = lax.all_to_all(out, B, 0, 0, tiled=True)  12.9 us
    pallas_call x1, Pallas kernels, on_device(): pl.pallas_call(spectral_kernel, out_shape=sds((NA * ROWS, LANES), bf16),...  4.21 us
    pallas_call x1, Pallas kernels, on_device(): pl.pallas_call(pack_kernel, out_shape=(sds((2 * ND, LANES), bf16), sds((6...  1.91 us

profile of v5, /device:TPU:1, one launch (start us, length us, event | category | flops | bytes accessed | tf_op | source)
XLA Modules:
  0.0 75.5 jit_solution(9378256381238956169)
XLA Ops:
  0.6 1.9 %pack.1 = (bf16[1024,128]{1,0:T(8,128)(2,1)S(1)}, bf16[64,512]{1,0:T(8,128)(2,1)S(1)}, f32[32,128]{1,0:T(8,128)S(1)}, f32[8,1024]{1,0:T(8,128)S(1)}, bf16[64,102...) custom-call(s32[2,2]{1,0:T(2,128)} %refs_0_.1, bf16[2,4,1024]{2,1,0:T(4,128)(2,1)} %refs_1_.1, ...), custom_call_target="tpu_custom_call" | custom-call | tf_op jit(solution)/shard_map/pack/pallas_call | solution.py:321
  2.5 0.0 copy-start
  2.6 0.0 copy-start.1
  2.6 0.0 copy-start.2
  2.6 38.7 %all_to_all.15 = bf16[512,2,128]{2,1,0:T(2,128)(2,1)S(1)} all-to-all(bf16[512,2,128]{2,1,0:T(2,128)(2,1)S(1)} %bitcast.8), channel_id=1, replica_groups=mesh['zh'=4,'zl'=2,'yl'=2,'c'=2,'x'=4,'yh'=4] {'x','yl','c','zh','zl','yh'}, dimensions={0} | all-to-all | bytes 524288 | tf_op jit(solution)/shard_map/all_to_all | solution.py:347
  41.3 4.2 %spectral.1 = bf16[832,128]{1,0:T(8,128)(2,1)S(1)} custom-call(bf16[1024,128]{1,0:T(8,128)(2,1)S(1)} %bitcast.5, f32[32,128]{1,0:T(8,128)S(1)} %get-tuple-element.9.gram, f32[8,1024]{1,0:T(8,128)S(1)} %get-tuple-element.10.lam, bf16[64,1024]{1,0:T(8,128)(2,1)S(1)} %get-tuple-element.11.first, bf16[64,128]{1,0:T(8,128)(2,1)S(1)} %get-tuple-element.12.second), custom_call_target="tpu_custom_call" | custom-call | tf_op jit(solution)/shard_map/spectral/pallas_call | solution.py:348
  45.5 15.9 %all_to_all.16 = bf16[32,13,2,128]{3,2,1,0:T(2,128)(2,1)S(1)} all-to-all(bf16[32,13,2,128]{3,2,1,0:T(2,128)(2,1)S(1)} %bitcast.7), channel_id=1, replica_groups=mesh['zh'=4,'zl'=2,'yl'=2,'c'=2,'x'=4,'yh'=4] {'zh','zl','yh'}, dimensions={0} | all-to-all | bytes 425984 | tf_op jit(solution)/shard_map/all_to_all | solution.py:360
  61.5 0.1 relay.1
  61.6 12.9 %all_to_all.17.got = bf16[16,64,128]{2,1,0:T(8,128)(2,1)S(1)} all-to-all(bf16[16,64,128]{2,1,0:T(8,128)(2,1)S(1)} %relay.1), channel_id=1, replica_groups=mesh['zh'=4,'zl'=2,'yl'=2,'c'=2,'x'=4,'yh'=4] {'x','yl','c'}, dimensions={0} | all-to-all | bytes 524288 | tf_op jit(solution)/shard_map/all_to_all | solution.py:370
  74.5 0.0 copy-done
  74.5 0.0 copy-done.1
  74.5 0.0 copy-done.2
  74.5 1.0 %finish.1 = (f32[2,512]{1,0:T(2,128)}, f32[32,32]{1,0:T(8,128)}) custom-call(bf16[16,64,128]{2,1,0:T(8,128)(2,1)S(1)} %all_to_all.17.got, bf16[64,512]{1,0:T(8,128)(2,1)S(1)} %get-tuple-element.13.pairs, bf16[2,16,1024]{2,1,0:T(8,128)(2,1)S(1)} %copy-done, bf16[2,512]{1,0:T(2,128)(2,1)S(1)} %copy-done.1, f32[2,16]{1,0:T(2,128)S(1)} %copy-done.2), custom_call_target="tpu_custom_call" | custom-call | tf_op jit(solution)/shard_map/finish/pallas_call | solution.py:371
Async XLA Ops:
  2.5 71.9 %copy-start = (bf16[2,16,1024]{2,1,0:T(8,128)(2,1)S(1)}, bf16[2,16,1024]{2,1,0:T(8,128)(2,1)}, u32[]{:S(2)}) copy-start(bf16[2,16,1024]{2,1,0:T(8,128)(2,1)} %pe.1) | copy-start | bytes 196612
  2.6 71.9 %copy-start.1 = (bf16[2,512]{1,0:T(2,128)(2,1)S(1)}, bf16[2,512]{1,0:T(2,128)(2,1)}, u32[]{:S(2)}) copy-start(bf16[2,512]{1,0:T(2,128)(2,1)} %vec.1) | copy-start | bytes 6148
  2.6 71.9 %copy-start.2 = (f32[2,16]{1,0:T(2,128)S(1)}, f32[2,16]{1,0:T(2,128)}, u32[]{:S(2)}) copy-start(f32[2,16]{1,0:T(2,128)} %energy.1) | copy-start | bytes 388

commit v6 on v5

--- a/solution.py
+++ b/solution.py
@@ -15,7 +15,7 @@
 NV = 32
 NT = NK * NB
 NQ = 289
-CHUNK = 256
+SPAN = NK // 4
 NAMES = ("zh", "zl", "yl", "c", "x", "yh")
 SIZES = (4, 2, 2, 2, 4, 4)
 A = ("zh", "zl", "yh")
@@ -44,14 +44,16 @@
     m = np.arange(32)
     phase = 2.0 * np.pi * ((m[:, None] * m[None, :]) % 32) / 32.0
     cas = np.cos(phase) + np.sin(phase)
-    first = split_table(np.repeat(cas, 32, axis=1))
-    second = split_table(np.tile(cas, (1, 4)) / 32.0)
+    first = split_table(np.repeat(cas[:, 0:16], 16, axis=1))
+    second = split_table(np.tile(cas[:, 0:16], (1, 8)) / 32.0)
     f = np.arange(17)
     weight = np.where((f == 0) | (f == 16), 1.0, 2.0)
     cos = weight[:, None] * np.cos(2.0 * np.pi * ((f[:, None] * m[None, :]) % 32) / 32.0)
-    outer = np.zeros((24, NK), np.float32)
-    outer[0:17] = np.repeat(cos, 32, axis=1)
-    inner = np.tile(cos, (17, 4)).astype(np.float32)
+    outer = np.zeros((24, 2 * SPAN), np.float32)
+    outer[0:17] = np.repeat(cos, 16, axis=1)
+    inner = np.concatenate(
+        [np.tile(cos[:, h : h + 16], (17, LANES // 16)) for h in (0, 16)], axis=1
+    ).astype(np.float32)
     return first, second, outer, inner
 
 
@@ -106,16 +108,28 @@
 
 def spectrum(lane_at, tiles, outer, inner):
     own = iota((NQ, LANES), 1) == lane_at
-    pick = jnp.where(iota((24, NQ), 0) == iota((24, NQ), 1) // 17, 1.0, 0.0)
-    out = []
+    pick = jnp.where(iota((24, NQ), 0) == iota((24, NQ), 1) // 17, 1.0, 0.0).astype(bf16)
+    parts = []
     for g in range(2):
         column = jnp.sum(jnp.where(own, tiles[g], 0.0), axis=1, keepdims=True)
-        part = jnp.dot(pick, column * inner[...], precision=HIGH, preferred_element_type=f32)
-        line = [
-            jnp.sum(outer[:, j * LANES : (j + 1) * LANES] * part, axis=0, keepdims=True)
-            for j in range(NK // LANES)
-        ]
-        out.append(jnp.concatenate(line, axis=1))
+        exact = column * inner[...]
+        hi = exact.astype(bf16)
+        lo = (exact - hi.astype(f32)).astype(bf16)
+        parts.append(
+            jnp.dot(pick, hi, preferred_element_type=f32)
+            + jnp.dot(pick, lo, preferred_element_type=f32)
+        )
+    out = []
+    for q in range(4):
+        for g in range(2):
+            part = parts[g][:, (q % 2) * LANES : (q % 2 + 1) * LANES]
+            line = []
+            for j in range(SPAN // LANES):
+                at = (q // 2) * SPAN + j * LANES
+                line.append(
+                    jnp.sum(outer[:, at : at + LANES] * part, axis=0, keepdims=True)
+                )
+            out.append(jnp.concatenate(line, axis=1))
     return out
 
 
@@ -170,56 +184,69 @@
     lines_of = spectrum(mine - tile, tiles, outer, inner)
     for g in range(2):
         factor = jnp.sum(jnp.where(index == mine + g * HALF, bare[...], 0.0), keepdims=True)
-        lines_of.append(jnp.broadcast_to(factor, (1, NK)))
-    lam[...] = jnp.concatenate(lines_of + [jnp.zeros((4, NK), f32)], axis=0)
+        lines_of.append(jnp.broadcast_to(factor, (1, SPAN)))
+    lam[...] = jnp.concatenate(lines_of + [jnp.zeros((6, SPAN), f32)], axis=0)
 
 
 def spectral_kernel(got, gram, lam, first, second, msg, lines, wide):
     lines[0 : 2 * ND, :] = got[...].astype(f32)
-    proj = jnp.transpose(lines[pl.ds(0, ND, stride=2), :]).astype(bf16)
+    proj = jnp.transpose(lines[pl.ds(0, ND, stride=2), :])
     rest = lines[pl.ds(1, ND, stride=2), :]
+    turned = jnp.transpose(rest)
     slot = iota((ND, 64), 1) % 32
-    at_first, from_second = [], []
+    left = iota((ND, LANES), 1) < 64
+    basis, sign = [], []
+    hat = None
     for k in range(2):
         at = [rest[:, 64 + 2 * k + s : 65 + 2 * k + s].astype(jnp.int32) for s in range(2)]
         ones = [jnp.where(slot == p, 1.0, 0.0).astype(bf16) for p in at]
-        at_first.append(ones[0])
+        ta = jnp.dot(ones[0], first[...], preferred_element_type=f32)
         tb = jnp.dot(ones[1], second[...], preferred_element_type=f32)
-        from_second.append(jnp.concatenate([tb] * (CHUNK // LANES), axis=1))
-    back = [None, None]
+        exact = ta * jnp.concatenate([tb] * (SPAN // LANES), axis=1)
+        hi = exact.astype(bf16)
+        lo = (exact - hi.astype(f32)).astype(bf16)
+        basis.append((hi, lo))
+        sa, sb = [(1 - 2 * (p % 2)).astype(f32) for p in at]
+        sign.append((sb, sa, sa * sb))
+        at = [turned[64 + 2 * k + s : 65 + 2 * k + s].astype(jnp.int32) for s in range(2)]
+        sa, sb = [(1 - 2 * (p % 2)).astype(f32) for p in at]
+        own = proj[k * 64 : (k + 1) * 64]
+        own = jnp.concatenate([own, own * sb, own * sa, own * (sa * sb)], axis=0).astype(bf16)
+        part = jnp.dot(own, hi, preferred_element_type=f32) + jnp.dot(
+            own, lo, preferred_element_type=f32
+        )
+        hat = part if hat is None else hat + part
+    scale = jnp.concatenate(
+        [jnp.broadcast_to(lam[r : r + 1, :], (32, SPAN)) for r in range(8)], axis=0
+    )
+    exact = hat * scale
+    scaled = exact.astype(bf16)
+    finer = (exact - scaled.astype(f32)).astype(bf16)
+    hat = hat.astype(bf16)
+    both = jnp.concatenate(
+        [v[q * 64 : (q + 1) * 64] for q in range(4) for v in (scaled, finer)], axis=0
+    )
+    back = []
+    for k in range(2):
+        sb, sa, sab = sign[k]
+        wide_r = dot_nt(basis[k][0], both)
+        r = wide_r[:, 0:LANES] + sb * wide_r[:, LANES : 2 * LANES]
+        r = r + sa * wide_r[:, 2 * LANES : 3 * LANES] + sab * wide_r[:, 3 * LANES : 4 * LANES]
+        small = dot_nt(basis[k][1], scaled)
+        r = r + jnp.where(left, 1.0, sb) * small[:, 0:LANES]
+        r = r + jnp.where(left, sa, sab) * small[:, LANES : 2 * LANES]
+        back.append(r + pltpu.roll(r, 64, 1))
+    back = jnp.where(left, back[0], back[1])
     direct = None
-    for m in range(0, NK, CHUNK):
-        hat = None
-        basis = []
-        for k in range(2):
-            ta = jnp.dot(at_first[k], first[:, m : m + CHUNK], preferred_element_type=f32)
-            exact = ta * from_second[k]
-            hi = exact.astype(bf16)
-            lo = (exact - hi.astype(f32)).astype(bf16)
-            basis.append((hi, lo))
-            mine = proj[k * 64 : (k + 1) * 64]
-            part = jnp.dot(mine, hi, preferred_element_type=f32) + jnp.dot(
-                mine, lo, preferred_element_type=f32
+    for g in range(2):
+        x, y = [
+            jnp.concatenate(
+                [v[q * 64 + g * 32 : q * 64 + g * 32 + 32] for q in range(4)], axis=1
             )
-            hat = part if hat is None else hat + part
-        scale = jnp.concatenate(
-            [jnp.broadcast_to(lam[g : g + 1, m : m + CHUNK], (32, CHUNK)) for g in range(2)], axis=0
-        )
-        exact = hat * scale
-        scaled = exact.astype(bf16)
-        finer = (exact - scaled.astype(f32)).astype(bf16)
-        hat = hat.astype(bf16)
-        both = jnp.concatenate([scaled, finer], axis=0)
-        again = jnp.concatenate([scaled, jnp.zeros((64, CHUNK), bf16)], axis=0)
-        for k in range(2):
-            part = dot_nt(basis[k][0], both) + dot_nt(basis[k][1], again)
-            back[k] = part if back[k] is None else back[k] + part
-        part = dot_nt(hat[0:32], jnp.concatenate([scaled[0:32]] * 4, axis=0)) + dot_nt(
-            hat[32:64], jnp.concatenate([scaled[32:64]] * 4, axis=0)
-        )
+            for v in (hat, scaled)
+        ]
+        part = dot_nt(x, jnp.concatenate([y] * 4, axis=0))
         direct = part if direct is None else direct + part
-    back = [r + pltpu.roll(r, 64, 1) for r in back]
-    back = jnp.where(iota((ND, LANES), 1) < 64, back[0], back[1])
     for b in range(NBB):
         lines[pl.ds(b, NA, stride=ROWS), :] = back[b * NA : (b + 1) * NA]
     lane = iota((1, LANES), 1)
@@ -227,7 +254,7 @@
     outer = jnp.zeros((32, LANES), f32)
     cd = jnp.zeros((1, LANES), f32)
     for g in range(2):
-        factor = lam[2 + g : 3 + g, 0:LANES]
+        factor = lam[8 + g : 9 + g, 0:LANES]
         own = jnp.where(lane // 32 == g, dens, 0.0)
         row = block_sum(own)
         column = jnp.sum(
@@ -324,8 +351,8 @@
             sds((2 * ND, LANES), bf16),
             sds((64, HALF), bf16),
             sds((32, LANES), f32),
-            sds((8, NK), f32),
-            sds((64, NK), bf16),
+            sds((16, SPAN), f32),
+            sds((64, SPAN), bf16),
             sds((64, LANES), bf16),
         ),
         in_specs=[any_space] * len(far),
@@ -334,8 +361,8 @@
         + [
             pltpu.VMEM((2, NQ, LANES), f32),
             pltpu.VMEM((8, LANES), f32),
-            pltpu.VMEM((24, NK), f32),
-            pltpu.VMEM((NQ, LANES), f32),
+            pltpu.VMEM((24, 2 * SPAN), f32),
+            pltpu.VMEM((NQ, 2 * LANES), f32),
             pltpu.VMEM((32, LANES), f32),
             pltpu.VMEM((64, HALF), f32),
             pltpu.VMEM((2 * ND, LANES), f32),

time: 75.7 us -> 73.5 us (0.971)
  Pallas kernels: 7.2 us -> 5.01 us
    pallas_call x1, Pallas kernels: 4.21 us -> 2.04 us  [on_device(): pl.pallas_call(spectral_kernel, out_shape=sds((NA * ROWS, LANES), bf16),...]
where the time goes in v6:
time: 73.5 us; the launch traced here: 73.3 us
  blocking collectives  67.6 us (92%)
  Pallas kernels  5.01 us (7%)
    all_to_all x1, blocking collectives, on_device(): got = lax.all_to_all(msg.reshape(ND, 2, LANES), B + A, 0, 0, tiled=True)  38.8 us
    all_to_all x1, blocking collectives, on_device(): lax.all_to_all(out.reshape(NA, ROWS // 2, 2, LANES), A, 0, 0, tiled=True)  16 us
    all_to_all x1, blocking collectives, on_device(): got = lax.all_to_all(out, B, 0, 0, tiled=True)  12.8 us
    pallas_call x1, Pallas kernels, on_device(): pl.pallas_call(spectral_kernel, out_shape=sds((NA * ROWS, LANES), bf16),...  2.04 us
    pallas_call x1, Pallas kernels, on_device(): pl.pallas_call(pack_kernel, out_shape=(sds((2 * ND, LANES), bf16), sds((6...  1.88 us

profile of v6, /device:TPU:1, one launch (start us, length us, event | category | flops | bytes accessed | tf_op | source)
XLA Modules:
  0.0 73.3 jit_solution(12314420525154105845)
XLA Ops:
  0.6 1.9 %pack.1 = (bf16[1024,128]{1,0:T(8,128)(2,1)S(1)}, bf16[64,512]{1,0:T(8,128)(2,1)S(1)}, f32[32,128]{1,0:T(8,128)S(1)}, f32[16,256]{1,0:T(8,128)S(1)}, bf16[64,256...) custom-call(s32[2,2]{1,0:T(2,128)} %refs_0_.1, bf16[2,4,1024]{2,1,0:T(4,128)(2,1)} %refs_1_.1, bf16[2,4,1024]{2,1,0:T(4,128)(2,1)} %refs_2_.1, ...), custom_call_target="tpu_custom_call" | custom-call | tf_op jit(solution)/shard_map/pack/pallas_call | solution.py:348
  2.5 0.0 copy-start
  2.5 0.0 copy-start.1
  2.5 0.0 copy-start.2
  2.6 38.8 %all_to_all.15 = bf16[512,2,128]{2,1,0:T(2,128)(2,1)S(1)} all-to-all(bf16[512,2,128]{2,1,0:T(2,128)(2,1)S(1)} %bitcast.8), channel_id=1, replica_groups=mesh['zh'=4,'zl'=2,'yl'=2,'c'=2,'x'=4,'yh'=4] {'x','yl','c','zh','zl','yh'}, dimensions={0} | all-to-all | bytes 524288 | tf_op jit(solution)/shard_map/all_to_all | solution.py:374
  41.3 2.0 %spectral.1 = bf16[832,128]{1,0:T(8,128)(2,1)S(1)} custom-call(bf16[1024,128]{1,0:T(8,128)(2,1)S(1)} %bitcast.5, f32[32,128]{1,0:T(8,128)S(1)} %get-tuple-element.9.gram, f32[16,256]{1,0:T(8,128)S(1)} %get-tuple-element.10.lam, bf16[64,256]{1,0:T(8,128)(2,1)S(1)} %get-tuple-element.11.first, bf16[64,128]{1,0:T(8,128)(2,1)S(1)} %get-tuple-element.12.second), custom_call_target="tpu_custom_call" | custom-call | tf_op jit(solution)/shard_map/spectral/pallas_call | solution.py:375
  43.4 16.0 %all_to_all.16 = bf16[32,13,2,128]{3,2,1,0:T(2,128)(2,1)S(1)} all-to-all(bf16[32,13,2,128]{3,2,1,0:T(2,128)(2,1)S(1)} %bitcast.6), channel_id=1, replica_groups=mesh['zh'=4,'zl'=2,'yl'=2,'c'=2,'x'=4,'yh'=4] {'zh','zl','yh'}, dimensions={0} | all-to-all | bytes 425984 | tf_op jit(solution)/shard_map/all_to_all | solution.py:387
  59.3 0.1 relay.1
  59.4 12.8 %all_to_all.17.got = bf16[16,64,128]{2,1,0:T(8,128)(2,1)S(1)} all-to-all(bf16[16,64,128]{2,1,0:T(8,128)(2,1)S(1)} %relay.1), channel_id=1, replica_groups=mesh['zh'=4,'zl'=2,'yl'=2,'c'=2,'x'=4,'yh'=4] {'x','yl','c'}, dimensions={0} | all-to-all | bytes 524288 | tf_op jit(solution)/shard_map/all_to_all | solution.py:397
  72.2 0.0 copy-done
  72.3 0.0 copy-done.1
  72.3 0.0 copy-done.2
  72.3 1.0 %finish.1 = (f32[2,512]{1,0:T(2,128)}, f32[32,32]{1,0:T(8,128)}) custom-call(bf16[16,64,128]{2,1,0:T(8,128)(2,1)S(1)} %all_to_all.17.got, bf16[64,512]{1,0:T(8,128)(2,1)S(1)} %get-tuple-element.13.pairs, bf16[2,16,1024]{2,1,0:T(8,128)(2,1)S(1)} %copy-done, bf16[2,512]{1,0:T(2,128)(2,1)S(1)} %copy-done.1, f32[2,16]{1,0:T(2,128)S(1)} %copy-done.2), custom_call_target="tpu_custom_call" | custom-call | tf_op jit(solution)/shard_map/finish/pallas_call | solution.py:398
Async XLA Ops:
  2.5 69.7 %copy-start = (bf16[2,16,1024]{2,1,0:T(8,128)(2,1)S(1)}, bf16[2,16,1024]{2,1,0:T(8,128)(2,1)}, u32[]{:S(2)}) copy-start(bf16[2,16,1024]{2,1,0:T(8,128)(2,1)} %pe.1) | copy-start | bytes 196612
  2.5 69.7 %copy-start.1 = (bf16[2,512]{1,0:T(2,128)(2,1)S(1)}, bf16[2,512]{1,0:T(2,128)(2,1)}, u32[]{:S(2)}) copy-start(bf16[2,512]{1,0:T(2,128)(2,1)} %vec.1) | copy-start | bytes 6148
  2.5 69.7 %copy-start.2 = (f32[2,16]{1,0:T(2,128)S(1)}, f32[2,16]{1,0:T(2,128)}, u32[]{:S(2)}) copy-start(f32[2,16]{1,0:T(2,128)} %energy.1) | copy-start | bytes 388

commit v7 on v6

--- a/solution.py
+++ b/solution.py
@@ -19,7 +19,7 @@
 NAMES = ("zh", "zl", "yl", "c", "x", "yh")
 SIZES = (4, 2, 2, 2, 4, 4)
 A = ("zh", "zl", "yh")
-B = ("x", "yl", "c")
+B = ("c", "x", "yl")
 NA = 32
 NBB = 16
 ND = NA * NBB
@@ -67,7 +67,7 @@
 
 
 def keep_block(x, wanted):
-    return jnp.where(iota(x.shape, 1) // 32 == wanted, x, 0.0)
+    return jnp.where(iota(x.shape, 1) >> 5 == wanted, x, 0.0)
 
 
 def spread_vectors(vec_ref, wide):
@@ -80,7 +80,7 @@
     for c in range(4):
         wide[pl.ds(c, 8, stride=4), :] = x8
     x = wide[...]
-    return block_sum(keep_block(x, iota(x.shape, 0) % 4))
+    return block_sum(keep_block(x, iota(x.shape, 0) & 3))
 
 
 def energy_column(energy_ref):
@@ -88,7 +88,7 @@
     second = jnp.broadcast_to(energy_ref[1:2, :], (NB, NB))
     e = jnp.concatenate([first, second], axis=0)
     return jnp.sum(
-        jnp.where(iota(e.shape, 1) == iota(e.shape, 0) % NB, e, 0.0), axis=1, keepdims=True
+        jnp.where(iota(e.shape, 1) == (iota(e.shape, 0) & (NB - 1)), e, 0.0), axis=1, keepdims=True
     )
 
 
@@ -134,8 +134,9 @@
 
 
 def pack_kernel(*refs):
-    far, (msg, pairs, gram, lam, first, second) = refs[:12], refs[12:18]
-    coords, cond, val, vec, pe, energy, tiles, bare, outer, inner, wide, rows, lines, sem = refs[18:]
+    far, (msg, pairs, gram), kept = refs[:12], refs[12:15], refs[15:21]
+    coords, cond, val, vec, pe, energy, wide, rows, lines, sem = refs[21:]
+    inner, outer, bare, first, second, tiles = kept
     mine = lax.axis_index(B) * NA + lax.axis_index(A)
     tile = pl.multiple_of((mine // LANES) * LANES, LANES)
     near = (coords, cond, val, vec, pe, energy, inner, outer, bare, first, second)
@@ -160,9 +161,9 @@
     left = rows[...].astype(bf16)
     pairs[...] = left
     xp = jnp.concatenate([x[0:16], x[0:16], x[16:32], x[16:32]], axis=0)
-    xp = keep_block(xp, iota(xp.shape, 0) // 16).astype(bf16)
+    xp = keep_block(xp, iota(xp.shape, 0) >> 4).astype(bf16)
     xd = jnp.concatenate([x, x], axis=0)
-    xd = keep_block(xd, iota(xd.shape, 0) // 32).astype(bf16)
+    xd = keep_block(xd, iota(xd.shape, 0) >> 5).astype(bf16)
     lane = iota((1, LANES), 1)
     place = jnp.zeros((1, LANES), f32)
     for k in range(2):
@@ -180,36 +181,42 @@
     )
     for copy in copies[6:]:
         copy.wait()
+
+
+def spectral_kernel(
+    got, gram, inner, outer_table, bare, first, second, tiles, msg, lines, wide
+):
+    mine = lax.axis_index(B) * NA + lax.axis_index(A)
+    lam = spectrum(mine % LANES, tiles, outer_table, inner)
     index = iota((8, LANES), 0) * LANES + iota((8, LANES), 1)
-    lines_of = spectrum(mine - tile, tiles, outer, inner)
-    for g in range(2):
-        factor = jnp.sum(jnp.where(index == mine + g * HALF, bare[...], 0.0), keepdims=True)
-        lines_of.append(jnp.broadcast_to(factor, (1, SPAN)))
-    lam[...] = jnp.concatenate(lines_of + [jnp.zeros((6, SPAN), f32)], axis=0)
-
-
-def spectral_kernel(got, gram, lam, first, second, msg, lines, wide):
+    factors = [
+        jnp.sum(jnp.where(index == mine + g * HALF, bare[...], 0.0), keepdims=True)
+        for g in range(2)
+    ]
     lines[0 : 2 * ND, :] = got[...].astype(f32)
     proj = jnp.transpose(lines[pl.ds(0, ND, stride=2), :])
     rest = lines[pl.ds(1, ND, stride=2), :]
     turned = jnp.transpose(rest)
-    slot = iota((ND, 64), 1) % 32
+    slot = iota((ND, 64), 1) & 31
     left = iota((ND, LANES), 1) < 64
     basis, sign = [], []
     hat = None
     for k in range(2):
-        at = [rest[:, 64 + 2 * k + s : 65 + 2 * k + s].astype(jnp.int32) for s in range(2)]
-        ones = [jnp.where(slot == p, 1.0, 0.0).astype(bf16) for p in at]
+        at = [
+            jnp.broadcast_to(rest[:, 64 + 2 * k + s : 65 + 2 * k + s], (ND, LANES)).astype(jnp.int32)
+            for s in range(2)
+        ]
+        ones = [jnp.where(slot == p[:, 0:64], 1.0, 0.0).astype(bf16) for p in at]
         ta = jnp.dot(ones[0], first[...], preferred_element_type=f32)
         tb = jnp.dot(ones[1], second[...], preferred_element_type=f32)
         exact = ta * jnp.concatenate([tb] * (SPAN // LANES), axis=1)
         hi = exact.astype(bf16)
         lo = (exact - hi.astype(f32)).astype(bf16)
         basis.append((hi, lo))
-        sa, sb = [(1 - 2 * (p % 2)).astype(f32) for p in at]
+        sa, sb = [jnp.where((p & 1) == 0, 1.0, -1.0) for p in at]
         sign.append((sb, sa, sa * sb))
         at = [turned[64 + 2 * k + s : 65 + 2 * k + s].astype(jnp.int32) for s in range(2)]
-        sa, sb = [(1 - 2 * (p % 2)).astype(f32) for p in at]
+        sa, sb = [jnp.where((p & 1) == 0, 1.0, -1.0) for p in at]
         own = proj[k * 64 : (k + 1) * 64]
         own = jnp.concatenate([own, own * sb, own * sa, own * (sa * sb)], axis=0).astype(bf16)
         part = jnp.dot(own, hi, preferred_element_type=f32) + jnp.dot(
@@ -217,7 +224,7 @@
         )
         hat = part if hat is None else hat + part
     scale = jnp.concatenate(
-        [jnp.broadcast_to(lam[r : r + 1, :], (32, SPAN)) for r in range(8)], axis=0
+        [jnp.broadcast_to(line, (32, SPAN)) for line in lam], axis=0
     )
     exact = hat * scale
     scaled = exact.astype(bf16)
@@ -254,8 +261,8 @@
     outer = jnp.zeros((32, LANES), f32)
     cd = jnp.zeros((1, LANES), f32)
     for g in range(2):
-        factor = lam[8 + g : 9 + g, 0:LANES]
-        own = jnp.where(lane // 32 == g, dens, 0.0)
+        factor = factors[g]
+        own = jnp.where(lane >> 5 == g, dens, 0.0)
         row = block_sum(own)
         column = jnp.sum(
             jnp.where(iota((32, LANES), 0) == iota((32, LANES), 1), row, 0.0), axis=1, keepdims=True
@@ -263,7 +270,7 @@
         outer = outer + column * (factor * row)
         cd = cd + factor * own
     alpha = (gram[...] + (2.0 / NT) * outer - direct / NK) / NT
-    wide[...] = keep_block(alpha, iota((32, LANES), 0) % 4)
+    wide[...] = keep_block(alpha, iota((32, LANES), 0) & 3)
     packed = wide[pl.ds(0, 8, stride=4), :]
     for c in range(1, 4):
         packed = packed + wide[pl.ds(c, 8, stride=4), :]
@@ -298,10 +305,10 @@
         field += [part, pltpu.roll(part, 64, 1)]
     field = jnp.concatenate(field, axis=0).astype(bf16)
     direct = jnp.dot(pairs[...], potential, preferred_element_type=f32)
-    direct = block_sum(keep_block(direct, iota(direct.shape, 0) // 16))
+    direct = block_sum(keep_block(direct, iota(direct.shape, 0) >> 4))
     direct = jnp.concatenate([direct[0:16] + direct[16:32], direct[32:48] + direct[48:64]], axis=0)
     exchange = jnp.dot(exchange_rows(pe), field, preferred_element_type=f32)
-    exchange = block_sum(keep_block(exchange, iota(exchange.shape, 0) // 32))
+    exchange = block_sum(keep_block(exchange, iota(exchange.shape, 0) >> 5))
     exchange = exchange[0:32] + exchange[32:64]
     applied = energy_column(energy) * x + (2.0 / NT) * exchange - direct / NK
     alpha = jnp.zeros((16, LANES), f32)
@@ -311,10 +318,10 @@
     for c in range(4):
         wide[pl.ds(c, 8, stride=4), :] = alpha
     full = wide[...]
-    full = block_sum(keep_block(full, iota(full.shape, 0) % 4))
+    full = block_sum(keep_block(full, iota(full.shape, 0) & 3))
     alpha_out[...] = full[:, 0:32]
     shift = jnp.dot(x[:, 0:32], full, precision=HIGH, preferred_element_type=f32)
-    rows[...] = keep_block(applied - shift, iota((32, LANES), 0) % 4)
+    rows[...] = keep_block(applied - shift, iota((32, LANES), 0) & 3)
     packed = rows[pl.ds(0, 8, stride=4), :]
     for c in range(1, 4):
         packed = packed + rows[pl.ds(c, 8, stride=4), :]
@@ -345,24 +352,23 @@
     far += (inner, outer, coulomb.reshape(8, LANES), first, second)
     any_space = pl.BlockSpec(memory_space=pl.ANY)
     own = [pltpu.VMEM(v.shape, v.dtype) for v in far[:6]]
-    msg, pairs, gram, lam, first, second = pl.pallas_call(
+    msg, pairs, gram, *kept = pl.pallas_call(
         pack_kernel,
         out_shape=(
             sds((2 * ND, LANES), bf16),
             sds((64, HALF), bf16),
             sds((32, LANES), f32),
-            sds((16, SPAN), f32),
+            sds((NQ, 2 * LANES), f32),
+            sds((24, 2 * SPAN), f32),
+            sds((8, LANES), f32),
             sds((64, SPAN), bf16),
             sds((64, LANES), bf16),
+            sds((2, NQ, LANES), f32),
         ),
         in_specs=[any_space] * len(far),
-        out_specs=(vmem(),) * 6,
+        out_specs=(vmem(),) * 9,
         scratch_shapes=own
         + [
-            pltpu.VMEM((2, NQ, LANES), f32),
-            pltpu.VMEM((8, LANES), f32),
-            pltpu.VMEM((24, 2 * SPAN), f32),
-            pltpu.VMEM((NQ, 2 * LANES), f32),
             pltpu.VMEM((32, LANES), f32),
             pltpu.VMEM((64, HALF), f32),
             pltpu.VMEM((2 * ND, LANES), f32),
@@ -375,7 +381,7 @@
     out = pl.pallas_call(
         spectral_kernel,
         out_shape=sds((NA * ROWS, LANES), bf16),
-        in_specs=[vmem()] * 5,
+        in_specs=[vmem()] * 8,
         out_specs=vmem(),
         scratch_shapes=[
             pltpu.VMEM((max(2 * ND, NA * ROWS), LANES), f32),
@@ -383,7 +389,7 @@
         ],
         compiler_params=room(28),
         name="spectral",
-    )(got.reshape(2 * ND, LANES), gram, lam, first, second)
+    )(got.reshape(2 * ND, LANES), gram, *kept)
     got = lax.all_to_all(out.reshape(NA, ROWS // 2, 2, LANES), A, 0, 0, tiled=True)
     out = pl.pallas_call(
         relay_kernel,

time: 73.5 us -> 72.8 us (level)
  no operation moved by 1% of the time
where the time goes in v7:
time: 72.8 us; the launch traced here: 72.6 us
  blocking collectives  67.1 us (92%)
  Pallas kernels  4.86 us (7%)
    all_to_all x1, blocking collectives, on_device(): got = lax.all_to_all(msg.reshape(ND, 2, LANES), B + A, 0, 0, tiled=True)  38.5 us
    all_to_all x1, blocking collectives, on_device(): lax.all_to_all(out.reshape(NA, ROWS // 2, 2, LANES), A, 0, 0, tiled=True)  15.9 us
    all_to_all x1, blocking collectives, on_device(): got = lax.all_to_all(out, B, 0, 0, tiled=True)  12.7 us
    pallas_call x1, Pallas kernels, on_device(): pl.pallas_call(spectral_kernel, out_shape=sds((NA * ROWS, LANES), bf16),...  2.28 us
    pallas_call x1, Pallas kernels, on_device(): pl.pallas_call(pack_kernel, out_shape=(sds((2 * ND, LANES), bf16), sds((6...  1.5 us

profile of v7, /device:TPU:1, one launch (start us, length us, event | category | flops | bytes accessed | tf_op | source)
XLA Modules:
  0.0 72.6 jit_solution(3994658258821445725)
XLA Ops:
  0.6 1.5 %pack.1 = (bf16[1024,128]{1,0:T(8,128)(2,1)S(1)}, bf16[64,512]{1,0:T(8,128)(2,1)S(1)}, f32[32,128]{1,0:T(8,128)S(1)}, f32[289,256]{1,0:T(8,128)S(1)}, f32[24,512...) custom-call(s32[2,2]{1,0:T(2,128)} %refs_0_.1, ...), custom_call_target="tpu_custom_call" | custom-call | tf_op jit(solution)/shard_map/pack/pallas_call | solution.py:355
  2.1 38.5 %all_to_all.15 = bf16[512,2,128]{2,1,0:T(2,128)(2,1)S(1)} all-to-all(bf16[512,2,128]{2,1,0:T(2,128)(2,1)S(1)} %bitcast.8), channel_id=1, replica_groups=mesh['zh'=4,'zl'=2,'yl'=2,'c'=2,'x'=4,'yh'=4] {'c','x','yl','zh','zl','yh'}, dimensions={0} | all-to-all | bytes 524288 | tf_op jit(solution)/shard_map/all_to_all | solution.py:380
  40.7 0.0 copy-start
  40.7 0.0 copy-start.1
  40.7 0.0 copy-start.2
  40.7 2.3 %spectral.1 = bf16[832,128]{1,0:T(8,128)(2,1)S(1)} custom-call(bf16[1024,128]{1,0:T(8,128)(2,1)S(1)} %bitcast.5, f32[32,128]{1,0:T(8,128)S(1)} %get-tuple-element.12.gram, f32[289,256]{1,0:T(8,128)S(1)} %get-tuple-element.13.inner, f32[24,512]{1,0:T(8,128)S(1)} %get-tuple-element.14.outer_table, f32[8,128]{1,0:T(8,128)S(1)} %get-tuple-element.15.bare, ...), custom_call_target="tpu_custom_call" | custom-call | tf_op jit(solution)/shard_map/spectral/pallas_call | solution.py:381
  43.0 15.9 %all_to_all.16 = bf16[32,13,2,128]{3,2,1,0:T(2,128)(2,1)S(1)} all-to-all(bf16[32,13,2,128]{3,2,1,0:T(2,128)(2,1)S(1)} %bitcast.6), channel_id=1, replica_groups=mesh['zh'=4,'zl'=2,'yl'=2,'c'=2,'x'=4,'yh'=4] {'zh','zl','yh'}, dimensions={0} | all-to-all | bytes 425984 | tf_op jit(solution)/shard_map/all_to_all | solution.py:393
  58.9 0.1 relay.1
  59.0 12.7 %all_to_all.17.got = bf16[16,64,128]{2,1,0:T(8,128)(2,1)S(1)} all-to-all(bf16[16,64,128]{2,1,0:T(8,128)(2,1)S(1)} %relay.1), channel_id=1, replica_groups=mesh['zh'=4,'zl'=2,'yl'=2,'c'=2,'x'=4,'yh'=4] {'c','x','yl'}, dimensions={0} | all-to-all | bytes 524288 | tf_op jit(solution)/shard_map/all_to_all | solution.py:403
  71.6 0.0 copy-done
  71.6 0.0 copy-done.1
  71.6 0.0 copy-done.2
  71.6 1.0 %finish.1 = (f32[2,512]{1,0:T(2,128)}, f32[32,32]{1,0:T(8,128)}) custom-call(bf16[16,64,128]{2,1,0:T(8,128)(2,1)S(1)} %all_to_all.17.got, bf16[64,512]{1,0:T(8,128)(2,1)S(1)} %get-tuple-element.19.pairs, bf16[2,16,1024]{2,1,0:T(8,128)(2,1)S(1)} %copy-done, bf16[2,512]{1,0:T(2,128)(2,1)S(1)} %copy-done.1, f32[2,16]{1,0:T(2,128)S(1)} %copy-done.2), custom_call_target="tpu_custom_call" | custom-call | tf_op jit(solution)/shard_map/finish/pallas_call | solution.py:404
Async XLA Ops:
  40.7 30.9 %copy-start = (bf16[2,16,1024]{2,1,0:T(8,128)(2,1)S(1)}, bf16[2,16,1024]{2,1,0:T(8,128)(2,1)}, u32[]{:S(2)}) copy-start(bf16[2,16,1024]{2,1,0:T(8,128)(2,1)} %pe.1) | copy-start | bytes 196612
  40.7 30.9 %copy-start.1 = (bf16[2,512]{1,0:T(2,128)(2,1)S(1)}, bf16[2,512]{1,0:T(2,128)(2,1)}, u32[]{:S(2)}) copy-start(bf16[2,512]{1,0:T(2,128)(2,1)} %vec.1) | copy-start | bytes 6148
  40.7 30.9 %copy-start.2 = (f32[2,16]{1,0:T(2,128)S(1)}, f32[2,16]{1,0:T(2,128)}, u32[]{:S(2)}) copy-start(f32[2,16]{1,0:T(2,128)} %energy.1) | copy-start | bytes 388

commit v8 on v7

--- a/solution.py
+++ b/solution.py
@@ -24,9 +24,9 @@
 NBB = 16
 ND = NA * NBB
 HALF = NG // 2
-ROWS = NBB + 10
+ROWS = NBB + 6
 FIELD = NA + NA // 2
-WIDE = FIELD + 16
+WIDE = FIELD + 8
 LANES = 128
 
 f32 = jnp.float32
@@ -183,6 +183,27 @@
         copy.wait()
 
 
+def fold(alpha):
+    n = iota((16, LANES), 1) & 31
+    row = iota((16, LANES), 0)
+    last = pltpu.roll(alpha[16:32], LANES - 16, 1)
+    half = jnp.where((row > n) & (n < 16), last, alpha[0:16])
+    corner = jnp.where(iota((16, LANES), 1) == row + 64, last, 0.0)
+    return half, jnp.sum(corner, axis=0, keepdims=True)
+
+
+def unfold(half, corner):
+    lane = iota((16, LANES), 1)
+    row = iota((16, LANES), 0)
+    half = jnp.where(lane < 32, half, 0.0)
+    turned = jnp.transpose(jnp.concatenate([half, jnp.zeros((LANES - 16, LANES), f32)], axis=0))
+    upper = jnp.where((lane < 16) & (row > lane), turned[0:16], half)
+    last = jnp.where(row > lane - 16, pltpu.roll(half, 16, 1), pltpu.roll(turned[0:16], 16, 1))
+    last = jnp.where(row == lane - 16, corner, last)
+    lower = jnp.where(lane < 16, turned[16:32], jnp.where(lane < 32, last, 0.0))
+    return block_sum(jnp.concatenate([upper, lower], axis=0))
+
+
 def spectral_kernel(
     got, gram, inner, outer_table, bare, first, second, tiles, msg, lines, wide
 ):
@@ -270,11 +291,12 @@
         outer = outer + column * (factor * row)
         cd = cd + factor * own
     alpha = (gram[...] + (2.0 / NT) * outer - direct / NK) / NT
-    wide[...] = keep_block(alpha, iota((32, LANES), 0) & 3)
-    packed = wide[pl.ds(0, 8, stride=4), :]
+    half, corner = fold(alpha)
+    wide[0:16, :] = keep_block(half, iota((16, LANES), 0) & 3)
+    packed = wide[pl.ds(0, 4, stride=4), :]
     for c in range(1, 4):
-        packed = packed + wide[pl.ds(c, 8, stride=4), :]
-    tail = jnp.concatenate([packed, cd, jnp.zeros((1, LANES), f32)], axis=0)
+        packed = packed + wide[pl.ds(c, 4, stride=4), :]
+    tail = jnp.concatenate([packed, cd + corner, jnp.zeros((1, LANES), f32)], axis=0)
     for r in range(ROWS - NBB):
         lines[pl.ds(NBB + r, NA, stride=ROWS), :] = jnp.broadcast_to(tail[r : r + 1], (NA, LANES))
     msg[...] = lines[0 : NA * ROWS, :].astype(bf16)
@@ -283,14 +305,22 @@
 def relay_kernel(got, msg, lines):
     lines[...] = got[...].astype(f32)
     alpha = []
-    for r in range(8):
+    for r in range(4):
         part = lines[pl.ds(NBB + r, NA, stride=ROWS), :]
         alpha.append(jnp.sum(part, axis=0, keepdims=True))
     alpha = jnp.concatenate(alpha, axis=0)
+    cd = lines[pl.ds(NBB + 4, NA, stride=ROWS), :]
+    corner = jnp.sum(cd, axis=0, keepdims=True)
+    cd = jnp.where(iota(cd.shape, 1) < 64, cd, 0.0)
+    cd = cd[0 : NA // 2] + pltpu.roll(cd[NA // 2 :], 64, 1)
     hi = alpha.astype(bf16).astype(f32)
-    cd = lines[pl.ds(NBB + 8, NA, stride=ROWS), :]
-    cd = cd[0 : NA // 2] + pltpu.roll(cd[NA // 2 :], 64, 1)
-    tail = jnp.concatenate([cd, hi, alpha - hi], axis=0).astype(bf16)
+    lane = iota((4, LANES), 1)
+    first = iota((4, LANES), 0) == 0
+    rough = corner.astype(bf16).astype(f32)
+    lo = jnp.where((lane & 31) < 16, alpha - hi, 0.0)
+    lo = jnp.where(first & (lane >> 4 == 1), pltpu.roll(rough, LANES - 48, 1), lo)
+    lo = jnp.where(first & (lane >> 4 == 3), pltpu.roll(corner - rough, LANES - 16, 1), lo)
+    tail = jnp.concatenate([cd, hi, lo], axis=0).astype(bf16)
     for b in range(NBB):
         msg[b, 0:NA, :] = lines[pl.ds(b, NA, stride=ROWS), :].astype(bf16)
         msg[b, NA:WIDE, :] = tail
@@ -311,14 +341,15 @@
     exchange = block_sum(keep_block(exchange, iota(exchange.shape, 0) >> 5))
     exchange = exchange[0:32] + exchange[32:64]
     applied = energy_column(energy) * x + (2.0 / NT) * exchange - direct / NK
-    alpha = jnp.zeros((16, LANES), f32)
+    alpha = jnp.zeros((8, LANES), f32)
     for b in range(NBB):
         alpha = alpha + got[b, FIELD:WIDE, :].astype(f32)
-    alpha = alpha[0:8] + alpha[8:16]
+    corner = alpha[4:5] + pltpu.roll(alpha[4:5], LANES - 32, 1)
+    half = alpha[0:4] + jnp.where((iota((4, LANES), 1) & 31) < 16, alpha[4:8], 0.0)
     for c in range(4):
-        wide[pl.ds(c, 8, stride=4), :] = alpha
-    full = wide[...]
-    full = block_sum(keep_block(full, iota(full.shape, 0) & 3))
+        wide[pl.ds(c, 4, stride=4), :] = half
+    full = wide[0:16, :]
+    full = unfold(block_sum(keep_block(full, iota(full.shape, 0) & 3)), corner)
     alpha_out[...] = full[:, 0:32]
     shift = jnp.dot(x[:, 0:32], full, precision=HIGH, preferred_element_type=f32)
     rows[...] = keep_block(applied - shift, iota((32, LANES), 0) & 3)

time: 72.8 us -> 72.1 us (level)
  blocking collectives: 67.1 us -> 66.1 us
    all_to_all x1, blocking collectives: 12.7 us -> 11.7 us  [on_device(): got = lax.all_to_all(out, B, 0, 0, tiled=True)]
where the time goes in v8:
time: 72.1 us; the launch traced here: 71.9 us
  blocking collectives  66.1 us (92%)
  Pallas kernels  5.2 us (7%)
    all_to_all x1, blocking collectives, on_device(): got = lax.all_to_all(msg.reshape(ND, 2, LANES), B + A, 0, 0, tiled=True)  38.5 us
    all_to_all x1, blocking collectives, on_device(): lax.all_to_all(out.reshape(NA, ROWS // 2, 2, LANES), A, 0, 0, tiled=True)  15.8 us
    all_to_all x1, blocking collectives, on_device(): got = lax.all_to_all(out, B, 0, 0, tiled=True)  11.7 us
    pallas_call x1, Pallas kernels, on_device(): pl.pallas_call(spectral_kernel, out_shape=sds((NA * ROWS, LANES), bf16),...  2.36 us
    pallas_call x1, Pallas kernels, on_device(): pl.pallas_call(pack_kernel, out_shape=(sds((2 * ND, LANES), bf16), sds((6...  1.5 us

profile of v8, /device:TPU:1, one launch (start us, length us, event | category | flops | bytes accessed | tf_op | source)
XLA Modules:
  0.0 71.9 jit_solution(17248092321493537610)
XLA Ops:
  0.6 1.5 %pack.1 = (bf16[1024,128]{1,0:T(8,128)(2,1)S(1)}, bf16[64,512]{1,0:T(8,128)(2,1)S(1)}, f32[32,128]{1,0:T(8,128)S(1)}, f32[289,256]{1,0:T(8,128)S(1)}, f32[24,512...) custom-call(s32[2,2]{1,0:T(2,128)} %refs_0_.1, ...), custom_call_target="tpu_custom_call" | custom-call | tf_op jit(solution)/shard_map/pack/pallas_call | solution.py:386
  2.1 38.5 %all_to_all.15 = bf16[512,2,128]{2,1,0:T(2,128)(2,1)S(1)} all-to-all(bf16[512,2,128]{2,1,0:T(2,128)(2,1)S(1)} %bitcast.8), channel_id=1, replica_groups=mesh['zh'=4,'zl'=2,'yl'=2,'c'=2,'x'=4,'yh'=4] {'c','x','yl','zh','zl','yh'}, dimensions={0} | all-to-all | bytes 524288 | tf_op jit(solution)/shard_map/all_to_all | solution.py:411
  40.7 0.0 copy-start
  40.7 0.0 copy-start.1
  40.7 0.0 copy-start.2
  40.7 2.4 %spectral.1 = bf16[704,128]{1,0:T(8,128)(2,1)S(1)} custom-call(bf16[1024,128]{1,0:T(8,128)(2,1)S(1)} %bitcast.5, f32[32,128]{1,0:T(8,128)S(1)} %get-tuple-element.12.gram, f32[289,256]{1,0:T(8,128)S(1)} %get-tuple-element.13.inner, f32[24,512]{1,0:T(8,128)S(1)} %get-tuple-element.14.outer_table, f32[8,128]{1,0:T(8,128)S(1)} %get-tuple-element.15.bare, ...), custom_call_target="tpu_custom_call" | custom-call | tf_op jit(solution)/shard_map/spectral/pallas_call | solution.py:412
  43.1 15.8 %all_to_all.16 = bf16[32,11,2,128]{3,2,1,0:T(2,128)(2,1)S(1)} all-to-all(bf16[32,11,2,128]{3,2,1,0:T(2,128)(2,1)S(1)} %bitcast.6), channel_id=1, replica_groups=mesh['zh'=4,'zl'=2,'yl'=2,'c'=2,'x'=4,'yh'=4] {'zh','zl','yh'}, dimensions={0} | all-to-all | bytes 360448 | tf_op jit(solution)/shard_map/all_to_all | solution.py:424
  58.8 0.1 relay.1
  58.9 11.7 %all_to_all.17.got = bf16[16,56,128]{2,1,0:T(8,128)(2,1)S(1)} all-to-all(bf16[16,56,128]{2,1,0:T(8,128)(2,1)S(1)} %relay.1), channel_id=1, replica_groups=mesh['zh'=4,'zl'=2,'yl'=2,'c'=2,'x'=4,'yh'=4] {'c','x','yl'}, dimensions={0} | all-to-all | bytes 458752 | tf_op jit(solution)/shard_map/all_to_all | solution.py:434
  70.7 0.0 copy-done
  70.7 0.0 copy-done.1
  70.7 0.0 copy-done.2
  70.7 1.2 %finish.1 = (f32[2,512]{1,0:T(2,128)}, f32[32,32]{1,0:T(8,128)}) custom-call(bf16[16,56,128]{2,1,0:T(8,128)(2,1)S(1)} %all_to_all.17.got, bf16[64,512]{1,0:T(8,128)(2,1)S(1)} %get-tuple-element.19.pairs, bf16[2,16,1024]{2,1,0:T(8,128)(2,1)S(1)} %copy-done, bf16[2,512]{1,0:T(2,128)(2,1)S(1)} %copy-done.1, f32[2,16]{1,0:T(2,128)S(1)} %copy-done.2), custom_call_target="tpu_custom_call" | custom-call | tf_op jit(solution)/shard_map/finish/pallas_call | solution.py:435
Async XLA Ops:
  40.7 30.0 %copy-start = (bf16[2,16,1024]{2,1,0:T(8,128)(2,1)S(1)}, bf16[2,16,1024]{2,1,0:T(8,128)(2,1)}, u32[]{:S(2)}) copy-start(bf16[2,16,1024]{2,1,0:T(8,128)(2,1)} %pe.1) | copy-start | bytes 196612
  40.7 30.0 %copy-start.1 = (bf16[2,512]{1,0:T(2,128)(2,1)S(1)}, bf16[2,512]{1,0:T(2,128)(2,1)}, u32[]{:S(2)}) copy-start(bf16[2,512]{1,0:T(2,128)(2,1)} %vec.1) | copy-start | bytes 6148
  40.7 30.0 %copy-start.2 = (f32[2,16]{1,0:T(2,128)S(1)}, f32[2,16]{1,0:T(2,128)}, u32[]{:S(2)}) copy-start(f32[2,16]{1,0:T(2,128)} %energy.1) | copy-start | bytes 388

commit v9 on v8

--- a/solution.py
+++ b/solution.py
@@ -31,7 +31,6 @@
 
 f32 = jnp.float32
 bf16 = jnp.bfloat16
-HIGH = lax.Precision.HIGHEST
 
 
 def split_table(x):
@@ -96,6 +95,11 @@
     return jnp.concatenate(
         [pe_ref[k, :, g * HALF : (g + 1) * HALF] for g in range(2) for k in range(2)], axis=0
     )
+
+
+def halves(x):
+    hi = x.astype(bf16)
+    return hi, (x - hi.astype(f32)).astype(bf16)
 
 
 def dot_t(x, y):
@@ -172,13 +176,9 @@
     lines[pl.ds(0, ND, stride=2), :] = dot_t(left, xp)
     lines[pl.ds(1, ND, stride=2), :] = dot_t(exchange_rows(pe), xd) + place
     msg[...] = lines[...].astype(bf16)
-    gram[...] = lax.dot_general(
-        x[:, 0:32],
-        energy_column(energy) * x,
-        (((0,), (0,)), ((), ())),
-        precision=HIGH,
-        preferred_element_type=f32,
-    )
+    hi, lo = halves(energy_column(energy) * x)
+    twice = jnp.concatenate([x, x], axis=0).astype(bf16)
+    gram[...] = dot_t(twice, jnp.concatenate([hi, lo], axis=0))[0:32]
     for copy in copies[6:]:
         copy.wait()
 
@@ -351,7 +351,12 @@
     full = wide[0:16, :]
     full = unfold(block_sum(keep_block(full, iota(full.shape, 0) & 3)), corner)
     alpha_out[...] = full[:, 0:32]
-    shift = jnp.dot(x[:, 0:32], full, precision=HIGH, preferred_element_type=f32)
+    none = jnp.zeros((64, LANES), bf16)
+    shift = jnp.dot(
+        x.astype(bf16),
+        jnp.concatenate([*halves(full), none], axis=0),
+        preferred_element_type=f32,
+    )
     rows[...] = keep_block(applied - shift, iota((32, LANES), 0) & 3)
     packed = rows[pl.ds(0, 8, stride=4), :]
     for c in range(1, 4):

time: 72.1 us -> 72.1 us (level)
  no operation moved by 1% of the time
where the time goes in v9:
time: 72.1 us; the launch traced here: 71.9 us
  blocking collectives  66.1 us (92%)
  Pallas kernels  5.14 us (7%)
    all_to_all x1, blocking collectives, on_device(): got = lax.all_to_all(msg.reshape(ND, 2, LANES), B + A, 0, 0, tiled=True)  38.5 us
    all_to_all x1, blocking collectives, on_device(): lax.all_to_all(out.reshape(NA, ROWS // 2, 2, LANES), A, 0, 0, tiled=True)  15.8 us
    all_to_all x1, blocking collectives, on_device(): got = lax.all_to_all(out, B, 0, 0, tiled=True)  11.7 us
    pallas_call x1, Pallas kernels, on_device(): pl.pallas_call(spectral_kernel, out_shape=sds((NA * ROWS, LANES), bf16),...  2.35 us
    pallas_call x1, Pallas kernels, on_device(): pl.pallas_call(pack_kernel, out_shape=(sds((2 * ND, LANES), bf16), sds((6...  1.49 us

profile of v9, /device:TPU:1, one launch (start us, length us, event | category | flops | bytes accessed | tf_op | source)
XLA Modules:
  0.0 71.9 jit_solution(15823223213708077437)
XLA Ops:
  0.6 1.5 %pack.1 = (bf16[1024,128]{1,0:T(8,128)(2,1)S(1)}, bf16[64,512]{1,0:T(8,128)(2,1)S(1)}, f32[32,128]{1,0:T(8,128)S(1)}, f32[289,256]{1,0:T(8,128)S(1)}, f32[24,512...) custom-call(s32[2,2]{1,0:T(2,128)} %refs_0_.1, ...), custom_call_target="tpu_custom_call" | custom-call | tf_op jit(solution)/shard_map/pack/pallas_call | solution.py:391
  2.1 38.5 %all_to_all.15 = bf16[512,2,128]{2,1,0:T(2,128)(2,1)S(1)} all-to-all(bf16[512,2,128]{2,1,0:T(2,128)(2,1)S(1)} %bitcast.8), channel_id=1, replica_groups=mesh['zh'=4,'zl'=2,'yl'=2,'c'=2,'x'=4,'yh'=4] {'c','x','yl','zh','zl','yh'}, dimensions={0} | all-to-all | bytes 524288 | tf_op jit(solution)/shard_map/all_to_all | solution.py:416
  40.7 0.0 copy-start
  40.7 0.0 copy-start.1
  40.7 0.0 copy-start.2
  40.7 2.4 %spectral.1 = bf16[704,128]{1,0:T(8,128)(2,1)S(1)} custom-call(bf16[1024,128]{1,0:T(8,128)(2,1)S(1)} %bitcast.5, f32[32,128]{1,0:T(8,128)S(1)} %get-tuple-element.12.gram, f32[289,256]{1,0:T(8,128)S(1)} %get-tuple-element.13.inner, f32[24,512]{1,0:T(8,128)S(1)} %get-tuple-element.14.outer_table, f32[8,128]{1,0:T(8,128)S(1)} %get-tuple-element.15.bare, ...), custom_call_target="tpu_custom_call" | custom-call | tf_op jit(solution)/shard_map/spectral/pallas_call | solution.py:417
  43.0 15.8 %all_to_all.16 = bf16[32,11,2,128]{3,2,1,0:T(2,128)(2,1)S(1)} all-to-all(bf16[32,11,2,128]{3,2,1,0:T(2,128)(2,1)S(1)} %bitcast.6), channel_id=1, replica_groups=mesh['zh'=4,'zl'=2,'yl'=2,'c'=2,'x'=4,'yh'=4] {'zh','zl','yh'}, dimensions={0} | all-to-all | bytes 360448 | tf_op jit(solution)/shard_map/all_to_all | solution.py:429
  58.8 0.1 relay.1
  59.0 11.7 %all_to_all.17.got = bf16[16,56,128]{2,1,0:T(8,128)(2,1)S(1)} all-to-all(bf16[16,56,128]{2,1,0:T(8,128)(2,1)S(1)} %relay.1), channel_id=1, replica_groups=mesh['zh'=4,'zl'=2,'yl'=2,'c'=2,'x'=4,'yh'=4] {'c','x','yl'}, dimensions={0} | all-to-all | bytes 458752 | tf_op jit(solution)/shard_map/all_to_all | solution.py:439
  70.7 0.0 copy-done
  70.7 0.0 copy-done.1
  70.7 0.0 copy-done.2
  70.7 1.2 %finish.1 = (f32[2,512]{1,0:T(2,128)}, f32[32,32]{1,0:T(8,128)}) custom-call(bf16[16,56,128]{2,1,0:T(8,128)(2,1)S(1)} %all_to_all.17.got, bf16[64,512]{1,0:T(8,128)(2,1)S(1)} %get-tuple-element.19.pairs, bf16[2,16,1024]{2,1,0:T(8,128)(2,1)S(1)} %copy-done, bf16[2,512]{1,0:T(2,128)(2,1)S(1)} %copy-done.1, f32[2,16]{1,0:T(2,128)S(1)} %copy-done.2), custom_call_target="tpu_custom_call" | custom-call | tf_op jit(solution)/shard_map/finish/pallas_call | solution.py:440
Async XLA Ops:
  40.7 30.0 %copy-start = (bf16[2,16,1024]{2,1,0:T(8,128)(2,1)S(1)}, bf16[2,16,1024]{2,1,0:T(8,128)(2,1)}, u32[]{:S(2)}) copy-start(bf16[2,16,1024]{2,1,0:T(8,128)(2,1)} %pe.1) | copy-start | bytes 196612
  40.7 30.0 %copy-start.1 = (bf16[2,512]{1,0:T(2,128)(2,1)S(1)}, bf16[2,512]{1,0:T(2,128)(2,1)}, u32[]{:S(2)}) copy-start(bf16[2,512]{1,0:T(2,128)(2,1)} %vec.1) | copy-start | bytes 6148
  40.7 30.0 %copy-start.2 = (f32[2,16]{1,0:T(2,128)S(1)}, f32[2,16]{1,0:T(2,128)}, u32[]{:S(2)}) copy-start(f32[2,16]{1,0:T(2,128)} %energy.1) | copy-start | bytes 388

commit v10 on v9

--- a/solution.py
+++ b/solution.py
@@ -18,8 +18,8 @@
 SPAN = NK // 4
 NAMES = ("zh", "zl", "yl", "c", "x", "yh")
 SIZES = (4, 2, 2, 2, 4, 4)
-A = ("zh", "zl", "yh")
-B = ("c", "x", "yl")
+A = ("yh", "yl", "zh")
+B = ("c", "x", "zl")
 NA = 32
 NBB = 16
 ND = NA * NBB
@@ -172,7 +172,9 @@
     place = jnp.zeros((1, LANES), f32)
     for k in range(2):
         for s in range(2):
-            place = jnp.where(lane == 64 + 2 * k + s, coords[k : k + 1, s : s + 1].astype(f32), place)
+            at = coords[k : k + 1, s : s + 1]
+            place = jnp.where(lane == 64 + 2 * k + s, at.astype(f32), place)
+            place = jnp.where(lane == 68 + 2 * k + s, (1 - 2 * (at & 1)).astype(f32), place)
     lines[pl.ds(0, ND, stride=2), :] = dot_t(left, xp)
     lines[pl.ds(1, ND, stride=2), :] = dot_t(exchange_rows(pe), xd) + place
     msg[...] = lines[...].astype(bf16)
@@ -218,26 +220,27 @@
     proj = jnp.transpose(lines[pl.ds(0, ND, stride=2), :])
     rest = lines[pl.ds(1, ND, stride=2), :]
     turned = jnp.transpose(rest)
-    slot = iota((ND, 64), 1) & 31
+    slot = (iota((ND, 64), 1) & 31).astype(f32)
     left = iota((ND, LANES), 1) < 64
     basis, sign = [], []
     hat = None
     for k in range(2):
-        at = [
-            jnp.broadcast_to(rest[:, 64 + 2 * k + s : 65 + 2 * k + s], (ND, LANES)).astype(jnp.int32)
+        ones = [
+            jnp.where(slot == rest[:, 64 + 2 * k + s : 65 + 2 * k + s], 1.0, 0.0).astype(bf16)
             for s in range(2)
         ]
-        ones = [jnp.where(slot == p[:, 0:64], 1.0, 0.0).astype(bf16) for p in at]
         ta = jnp.dot(ones[0], first[...], preferred_element_type=f32)
         tb = jnp.dot(ones[1], second[...], preferred_element_type=f32)
         exact = ta * jnp.concatenate([tb] * (SPAN // LANES), axis=1)
         hi = exact.astype(bf16)
         lo = (exact - hi.astype(f32)).astype(bf16)
         basis.append((hi, lo))
-        sa, sb = [jnp.where((p & 1) == 0, 1.0, -1.0) for p in at]
+        sa, sb = [
+            jnp.broadcast_to(rest[:, 68 + 2 * k + s : 69 + 2 * k + s], (ND, LANES))
+            for s in range(2)
+        ]
         sign.append((sb, sa, sa * sb))
-        at = [turned[64 + 2 * k + s : 65 + 2 * k + s].astype(jnp.int32) for s in range(2)]
-        sa, sb = [jnp.where((p & 1) == 0, 1.0, -1.0) for p in at]
+        sa, sb = [turned[68 + 2 * k + s : 69 + 2 * k + s] for s in range(2)]
         own = proj[k * 64 : (k + 1) * 64]
         own = jnp.concatenate([own, own * sb, own * sa, own * (sa * sb)], axis=0).astype(bf16)
         part = jnp.dot(own, hi, preferred_element_type=f32) + jnp.dot(

time: 72.1 us -> 71.8 us (level)
  blocking collectives: 66.1 us -> 65.3 us
    all_to_all x1, blocking collectives: 11.7 us -> 10.9 us  [on_device(): got = lax.all_to_all(out, B, 0, 0, tiled=True)]
where the time goes in v10:
time: 71.8 us; the launch traced here: 71 us
  blocking collectives  65.3 us (91%)
  Pallas kernels  5.03 us (7%)
    all_to_all x1, blocking collectives, on_device(): got = lax.all_to_all(msg.reshape(ND, 2, LANES), B + A, 0, 0, tiled=True)  39.1 us
    all_to_all x1, blocking collectives, on_device(): lax.all_to_all(out.reshape(NA, ROWS // 2, 2, LANES), A, 0, 0, tiled=True)  15.3 us
    all_to_all x1, blocking collectives, on_device(): got = lax.all_to_all(out, B, 0, 0, tiled=True)  10.9 us
    pallas_call x1, Pallas kernels, on_device(): pl.pallas_call(spectral_kernel, out_shape=sds((NA * ROWS, LANES), bf16),...  2.24 us
    pallas_call x1, Pallas kernels, on_device(): pl.pallas_call(pack_kernel, out_shape=(sds((2 * ND, LANES), bf16), sds((6...  1.49 us

profile of v10, /device:TPU:1, one launch (start us, length us, event | category | flops | bytes accessed | tf_op | source)
XLA Modules:
  0.0 71.0 jit_solution(13144600616288280637)
XLA Ops:
  0.6 1.5 %pack.1 = (bf16[1024,128]{1,0:T(8,128)(2,1)S(1)}, bf16[64,512]{1,0:T(8,128)(2,1)S(1)}, f32[32,128]{1,0:T(8,128)S(1)}, f32[289,256]{1,0:T(8,128)S(1)}, f32[24,512...) custom-call(s32[2,2]{1,0:T(2,128)} %refs_0_.1, ...), custom_call_target="tpu_custom_call" | custom-call | tf_op jit(solution)/shard_map/pack/pallas_call | solution.py:394
  2.1 39.1 %all_to_all.15 = bf16[512,2,128]{2,1,0:T(2,128)(2,1)S(1)} all-to-all(bf16[512,2,128]{2,1,0:T(2,128)(2,1)S(1)} %bitcast.8), channel_id=1, replica_groups=mesh['zh'=4,'zl'=2,'yl'=2,'c'=2,'x'=4,'yh'=4] {'c','x','zl','yh','yl','zh'}, dimensions={0} | all-to-all | bytes 524288 | tf_op jit(solution)/shard_map/all_to_all | solution.py:419
  41.2 0.0 copy-start
  41.2 0.0 copy-start.1
  41.2 0.0 copy-start.2
  41.2 2.2 %spectral.1 = bf16[704,128]{1,0:T(8,128)(2,1)S(1)} custom-call(bf16[1024,128]{1,0:T(8,128)(2,1)S(1)} %bitcast.5, f32[32,128]{1,0:T(8,128)S(1)} %get-tuple-element.12.gram, f32[289,256]{1,0:T(8,128)S(1)} %get-tuple-element.13.inner, f32[24,512]{1,0:T(8,128)S(1)} %get-tuple-element.14.outer_table, f32[8,128]{1,0:T(8,128)S(1)} %get-tuple-element.15.bare, ...), custom_call_target="tpu_custom_call" | custom-call | tf_op jit(solution)/shard_map/spectral/pallas_call | solution.py:420
  43.5 15.3 %all_to_all.16 = bf16[32,11,2,128]{3,2,1,0:T(2,128)(2,1)S(1)} all-to-all(bf16[32,11,2,128]{3,2,1,0:T(2,128)(2,1)S(1)} %bitcast.6), channel_id=1, replica_groups=mesh['zh'=4,'zl'=2,'yl'=2,'c'=2,'x'=4,'yh'=4] {'yh','yl','zh'}, dimensions={0} | all-to-all | bytes 360448 | tf_op jit(solution)/shard_map/all_to_all | solution.py:432
  58.8 0.1 relay.1
  58.9 10.9 %all_to_all.17.got = bf16[16,56,128]{2,1,0:T(8,128)(2,1)S(1)} all-to-all(bf16[16,56,128]{2,1,0:T(8,128)(2,1)S(1)} %relay.1), channel_id=1, replica_groups=mesh['zh'=4,'zl'=2,'yl'=2,'c'=2,'x'=4,'yh'=4] {'c','x','zl'}, dimensions={0} | all-to-all | bytes 458752 | tf_op jit(solution)/shard_map/all_to_all | solution.py:442
  69.8 0.0 copy-done
  69.8 0.0 copy-done.1
  69.8 0.0 copy-done.2
  69.8 1.2 %finish.1 = (f32[2,512]{1,0:T(2,128)}, f32[32,32]{1,0:T(8,128)}) custom-call(bf16[16,56,128]{2,1,0:T(8,128)(2,1)S(1)} %all_to_all.17.got, bf16[64,512]{1,0:T(8,128)(2,1)S(1)} %get-tuple-element.19.pairs, bf16[2,16,1024]{2,1,0:T(8,128)(2,1)S(1)} %copy-done, bf16[2,512]{1,0:T(2,128)(2,1)S(1)} %copy-done.1, f32[2,16]{1,0:T(2,128)S(1)} %copy-done.2), custom_call_target="tpu_custom_call" | custom-call | tf_op jit(solution)/shard_map/finish/pallas_call | solution.py:443
Async XLA Ops:
  41.2 28.6 %copy-start = (bf16[2,16,1024]{2,1,0:T(8,128)(2,1)S(1)}, bf16[2,16,1024]{2,1,0:T(8,128)(2,1)}, u32[]{:S(2)}) copy-start(bf16[2,16,1024]{2,1,0:T(8,128)(2,1)} %pe.1) | copy-start | bytes 196612
  41.2 28.6 %copy-start.1 = (bf16[2,512]{1,0:T(2,128)(2,1)S(1)}, bf16[2,512]{1,0:T(2,128)(2,1)}, u32[]{:S(2)}) copy-start(bf16[2,512]{1,0:T(2,128)(2,1)} %vec.1) | copy-start | bytes 6148
  41.2 28.6 %copy-start.2 = (f32[2,16]{1,0:T(2,128)S(1)}, f32[2,16]{1,0:T(2,128)}, u32[]{:S(2)}) copy-start(f32[2,16]{1,0:T(2,128)} %energy.1) | copy-start | bytes 388

commit v11 on v10

--- a/solution.py
+++ b/solution.py
@@ -151,7 +151,7 @@
     ]
     for copy in copies:
         copy.start()
-    for copy in copies[:6]:
+    for copy in copies[:4]:
         copy.wait()
     x = spread_vectors(vec, wide)
     for k in range(2):
@@ -176,6 +176,8 @@
             place = jnp.where(lane == 64 + 2 * k + s, at.astype(f32), place)
             place = jnp.where(lane == 68 + 2 * k + s, (1 - 2 * (at & 1)).astype(f32), place)
     lines[pl.ds(0, ND, stride=2), :] = dot_t(left, xp)
+    for copy in copies[4:6]:
+        copy.wait()
     lines[pl.ds(1, ND, stride=2), :] = dot_t(exchange_rows(pe), xd) + place
     msg[...] = lines[...].astype(bf16)
     hi, lo = halves(energy_column(energy) * x)

time: 71.8 us -> 71.8 us (level)
  no operation moved by 1% of the time
where the time goes in v11:
time: 71.8 us; the launch traced here: 71 us
  blocking collectives  65.3 us (91%)
  Pallas kernels  5.05 us (7%)
    all_to_all x1, blocking collectives, on_device(): got = lax.all_to_all(msg.reshape(ND, 2, LANES), B + A, 0, 0, tiled=True)  39.1 us
    all_to_all x1, blocking collectives, on_device(): lax.all_to_all(out.reshape(NA, ROWS // 2, 2, LANES), A, 0, 0, tiled=True)  15.3 us
    all_to_all x1, blocking collectives, on_device(): got = lax.all_to_all(out, B, 0, 0, tiled=True)  10.9 us
    pallas_call x1, Pallas kernels, on_device(): pl.pallas_call(spectral_kernel, out_shape=sds((NA * ROWS, LANES), bf16),...  2.24 us
    pallas_call x1, Pallas kernels, on_device(): pl.pallas_call(pack_kernel, out_shape=(sds((2 * ND, LANES), bf16), sds((6...  1.52 us

profile of v11, /device:TPU:1, one launch (start us, length us, event | category | flops | bytes accessed | tf_op | source)
XLA Modules:
  0.0 71.0 jit_solution(15292212739016257168)
XLA Ops:
  0.6 1.5 %pack.1 = (bf16[1024,128]{1,0:T(8,128)(2,1)S(1)}, bf16[64,512]{1,0:T(8,128)(2,1)S(1)}, f32[32,128]{1,0:T(8,128)S(1)}, f32[289,256]{1,0:T(8,128)S(1)}, f32[24,512...) custom-call(s32[2,2]{1,0:T(2,128)} %refs_0_.1, ...), custom_call_target="tpu_custom_call" | custom-call | tf_op jit(solution)/shard_map/pack/pallas_call | solution.py:396
  2.2 39.1 %all_to_all.15 = bf16[512,2,128]{2,1,0:T(2,128)(2,1)S(1)} all-to-all(bf16[512,2,128]{2,1,0:T(2,128)(2,1)S(1)} %bitcast.8), channel_id=1, replica_groups=mesh['zh'=4,'zl'=2,'yl'=2,'c'=2,'x'=4,'yh'=4] {'c','x','zl','yh','yl','zh'}, dimensions={0} | all-to-all | bytes 524288 | tf_op jit(solution)/shard_map/all_to_all | solution.py:421
  41.3 0.0 copy-start
  41.3 0.0 copy-start.1
  41.3 0.0 copy-start.2
  41.3 2.2 %spectral.1 = bf16[704,128]{1,0:T(8,128)(2,1)S(1)} custom-call(bf16[1024,128]{1,0:T(8,128)(2,1)S(1)} %bitcast.5, f32[32,128]{1,0:T(8,128)S(1)} %get-tuple-element.12.gram, f32[289,256]{1,0:T(8,128)S(1)} %get-tuple-element.13.inner, f32[24,512]{1,0:T(8,128)S(1)} %get-tuple-element.14.outer_table, f32[8,128]{1,0:T(8,128)S(1)} %get-tuple-element.15.bare, ...), custom_call_target="tpu_custom_call" | custom-call | tf_op jit(solution)/shard_map/spectral/pallas_call | solution.py:422
  43.5 15.3 %all_to_all.16 = bf16[32,11,2,128]{3,2,1,0:T(2,128)(2,1)S(1)} all-to-all(bf16[32,11,2,128]{3,2,1,0:T(2,128)(2,1)S(1)} %bitcast.6), channel_id=1, replica_groups=mesh['zh'=4,'zl'=2,'yl'=2,'c'=2,'x'=4,'yh'=4] {'yh','yl','zh'}, dimensions={0} | all-to-all | bytes 360448 | tf_op jit(solution)/shard_map/all_to_all | solution.py:434
  58.8 0.1 relay.1
  58.9 10.9 %all_to_all.17.got = bf16[16,56,128]{2,1,0:T(8,128)(2,1)S(1)} all-to-all(bf16[16,56,128]{2,1,0:T(8,128)(2,1)S(1)} %relay.1), channel_id=1, replica_groups=mesh['zh'=4,'zl'=2,'yl'=2,'c'=2,'x'=4,'yh'=4] {'c','x','zl'}, dimensions={0} | all-to-all | bytes 458752 | tf_op jit(solution)/shard_map/all_to_all | solution.py:444
  69.8 0.0 copy-done
  69.8 0.0 copy-done.1
  69.8 0.0 copy-done.2
  69.8 1.2 %finish.1 = (f32[2,512]{1,0:T(2,128)}, f32[32,32]{1,0:T(8,128)}) custom-call(bf16[16,56,128]{2,1,0:T(8,128)(2,1)S(1)} %all_to_all.17.got, bf16[64,512]{1,0:T(8,128)(2,1)S(1)} %get-tuple-element.19.pairs, bf16[2,16,1024]{2,1,0:T(8,128)(2,1)S(1)} %copy-done, bf16[2,512]{1,0:T(2,128)(2,1)S(1)} %copy-done.1, f32[2,16]{1,0:T(2,128)S(1)} %copy-done.2), custom_call_target="tpu_custom_call" | custom-call | tf_op jit(solution)/shard_map/finish/pallas_call | solution.py:445
Async XLA Ops:
  41.3 28.6 %copy-start = (bf16[2,16,1024]{2,1,0:T(8,128)(2,1)S(1)}, bf16[2,16,1024]{2,1,0:T(8,128)(2,1)}, u32[]{:S(2)}) copy-start(bf16[2,16,1024]{2,1,0:T(8,128)(2,1)} %pe.1) | copy-start | bytes 196612
  41.3 28.6 %copy-start.1 = (bf16[2,512]{1,0:T(2,128)(2,1)S(1)}, bf16[2,512]{1,0:T(2,128)(2,1)}, u32[]{:S(2)}) copy-start(bf16[2,512]{1,0:T(2,128)(2,1)} %vec.1) | copy-start | bytes 6148
  41.3 28.6 %copy-start.2 = (f32[2,16]{1,0:T(2,128)S(1)}, f32[2,16]{1,0:T(2,128)}, u32[]{:S(2)}) copy-start(f32[2,16]{1,0:T(2,128)} %energy.1) | copy-start | bytes 388

commit v12 on v10

--- a/solution.py
+++ b/solution.py
@@ -18,7 +18,7 @@
 SPAN = NK // 4
 NAMES = ("zh", "zl", "yl", "c", "x", "yh")
 SIZES = (4, 2, 2, 2, 4, 4)
-A = ("yh", "yl", "zh")
+A = ("zh", "yh", "yl")
 B = ("c", "x", "zl")
 NA = 32
 NBB = 16

time: 71.8 us -> 72.1 us (level)
  blocking collectives: 65.3 us -> 66.2 us
where the time goes in v12:
time: 72.1 us; the launch traced here: 71.9 us
  blocking collectives  66.2 us (92%)
  Pallas kernels  5.02 us (7%)
    all_to_all x1, blocking collectives, on_device(): got = lax.all_to_all(msg.reshape(ND, 2, LANES), B + A, 0, 0, tiled=True)  39.2 us
    all_to_all x1, blocking collectives, on_device(): lax.all_to_all(out.reshape(NA, ROWS // 2, 2, LANES), A, 0, 0, tiled=True)  15.6 us
    all_to_all x1, blocking collectives, on_device(): got = lax.all_to_all(out, B, 0, 0, tiled=True)  11.4 us
    pallas_call x1, Pallas kernels, on_device(): pl.pallas_call(spectral_kernel, out_shape=sds((NA * ROWS, LANES), bf16),...  2.23 us
    pallas_call x1, Pallas kernels, on_device(): pl.pallas_call(pack_kernel, out_shape=(sds((2 * ND, LANES), bf16), sds((6...  1.49 us

profile of v12, /device:TPU:1, one launch (start us, length us, event | category | flops | bytes accessed | tf_op | source)
XLA Modules:
  0.0 71.9 jit_solution(1862731475652815568)
XLA Ops:
  0.6 1.5 %pack.1 = (bf16[1024,128]{1,0:T(8,128)(2,1)S(1)}, bf16[64,512]{1,0:T(8,128)(2,1)S(1)}, f32[32,128]{1,0:T(8,128)S(1)}, f32[289,256]{1,0:T(8,128)S(1)}, f32[24,512...) custom-call(s32[2,2]{1,0:T(2,128)} %refs_0_.1, ...), custom_call_target="tpu_custom_call" | custom-call | tf_op jit(solution)/shard_map/pack/pallas_call | solution.py:394
  2.1 39.2 %all_to_all.15 = bf16[512,2,128]{2,1,0:T(2,128)(2,1)S(1)} all-to-all(bf16[512,2,128]{2,1,0:T(2,128)(2,1)S(1)} %bitcast.8), channel_id=1, replica_groups=mesh['zh'=4,'zl'=2,'yl'=2,'c'=2,'x'=4,'yh'=4] {'c','x','zl','zh','yh','yl'}, dimensions={0} | all-to-all | bytes 524288 | tf_op jit(solution)/shard_map/all_to_all | solution.py:419
  41.4 0.0 copy-start
  41.4 0.0 copy-start.1
  41.4 0.0 copy-start.2
  41.4 2.2 %spectral.1 = bf16[704,128]{1,0:T(8,128)(2,1)S(1)} custom-call(bf16[1024,128]{1,0:T(8,128)(2,1)S(1)} %bitcast.5, f32[32,128]{1,0:T(8,128)S(1)} %get-tuple-element.12.gram, f32[289,256]{1,0:T(8,128)S(1)} %get-tuple-element.13.inner, f32[24,512]{1,0:T(8,128)S(1)} %get-tuple-element.14.outer_table, f32[8,128]{1,0:T(8,128)S(1)} %get-tuple-element.15.bare, ...), custom_call_target="tpu_custom_call" | custom-call | tf_op jit(solution)/shard_map/spectral/pallas_call | solution.py:420
  43.6 15.6 %all_to_all.16 = bf16[32,11,2,128]{3,2,1,0:T(2,128)(2,1)S(1)} all-to-all(bf16[32,11,2,128]{3,2,1,0:T(2,128)(2,1)S(1)} %bitcast.6), channel_id=1, replica_groups=mesh['zh'=4,'zl'=2,'yl'=2,'c'=2,'x'=4,'yh'=4] {'zh','yh','yl'}, dimensions={0} | all-to-all | bytes 360448 | tf_op jit(solution)/shard_map/all_to_all | solution.py:432
  59.2 0.1 relay.1
  59.3 11.4 %all_to_all.17.got = bf16[16,56,128]{2,1,0:T(8,128)(2,1)S(1)} all-to-all(bf16[16,56,128]{2,1,0:T(8,128)(2,1)S(1)} %relay.1), channel_id=1, replica_groups=mesh['zh'=4,'zl'=2,'yl'=2,'c'=2,'x'=4,'yh'=4] {'c','x','zl'}, dimensions={0} | all-to-all | bytes 458752 | tf_op jit(solution)/shard_map/all_to_all | solution.py:442
  70.7 0.0 copy-done
  70.7 0.0 copy-done.1
  70.7 0.0 copy-done.2
  70.7 1.2 %finish.1 = (f32[2,512]{1,0:T(2,128)}, f32[32,32]{1,0:T(8,128)}) custom-call(bf16[16,56,128]{2,1,0:T(8,128)(2,1)S(1)} %all_to_all.17.got, bf16[64,512]{1,0:T(8,128)(2,1)S(1)} %get-tuple-element.19.pairs, bf16[2,16,1024]{2,1,0:T(8,128)(2,1)S(1)} %copy-done, bf16[2,512]{1,0:T(2,128)(2,1)S(1)} %copy-done.1, f32[2,16]{1,0:T(2,128)S(1)} %copy-done.2), custom_call_target="tpu_custom_call" | custom-call | tf_op jit(solution)/shard_map/finish/pallas_call | solution.py:443
Async XLA Ops:
  41.4 29.4 %copy-start = (bf16[2,16,1024]{2,1,0:T(8,128)(2,1)S(1)}, bf16[2,16,1024]{2,1,0:T(8,128)(2,1)}, u32[]{:S(2)}) copy-start(bf16[2,16,1024]{2,1,0:T(8,128)(2,1)} %pe.1) | copy-start | bytes 196612
  41.4 29.4 %copy-start.1 = (bf16[2,512]{1,0:T(2,128)(2,1)S(1)}, bf16[2,512]{1,0:T(2,128)(2,1)}, u32[]{:S(2)}) copy-start(bf16[2,512]{1,0:T(2,128)(2,1)} %vec.1) | copy-start | bytes 6148
  41.4 29.4 %copy-start.2 = (f32[2,16]{1,0:T(2,128)S(1)}, f32[2,16]{1,0:T(2,128)}, u32[]{:S(2)}) copy-start(f32[2,16]{1,0:T(2,128)} %energy.1) | copy-start | bytes 388
